TPU v7x, 32 devices: a whole 2x2x4 slice. The times are simulated.
32 devices in a mesh: bngroup: 4 (over z), rep: 8 (over y, x, core).
Axes of the slice: x: 2, y: 2, z: 4, core: 2. Of those that a mesh axis runs over, the one named last changes fastest.
Arguments:
- images: bfloat16 [384, 7, 7, 2048], P(('bngroup', 'rep')), may hold values from -12 to 12
- cotangent: bfloat16 [384, 7, 7, 2048], P(('bngroup', 'rep')), may hold values from -6 to 6
- w_reduce: bfloat16 [2048, 512], replicated, may hold values from -0.125 to 0.125
- w_spatial: bfloat16 [4608, 512], replicated, may hold values from -0.09375 to 0.09375
- w_expand: bfloat16 [2048, 512], replicated, may hold values from -0.25 to 0.25
- norm_gain: float32 [3072], replicated, may hold values from 0.25 to 1.75
- norm_shift: float32 [3072], replicated, may hold values from -3 to 3
Outputs:
- output: bfloat16 [384, 7, 7, 2048], P(('bngroup', 'rep'))
- in_grad: bfloat16 [384, 7, 7, 2048], P(('bngroup', 'rep'))
- weight_grads: float32 [8704, 512], P('bngroup', 'rep')
- norm_grads: float32 [2, 3072], replicated
All inputs are finite; a program needn't handle non-finite values.
Results may differ from a plain program's by a relative error of at most 0.007.
Values sent between devices are 32-bit elements.
A program may use at most 192 MiB of HBM per device.

v0:
```python
import jax
import jax.numpy as jnp
from jax import lax
from jax.sharding import PartitionSpec as P

EPS = 0.25


def matmul(left, right):
    return jnp.dot(left, right, preferred_element_type=jnp.float32)


def contract(left, right, left_dim, right_dim):
    return lax.dot_general(
        left, right, (((left_dim,), (right_dim,)), ((), ())), preferred_element_type=jnp.float32
    )


def slope(value):
    sigma = jax.nn.sigmoid(value)
    return sigma * (1.0 + value * (1.0 - sigma))


def normalize(pre_norm, norm_gain, norm_shift, group_size):
    number = pre_norm.shape[0] * group_size
    first_sum, second_sum = lax.psum(
        (jnp.sum(pre_norm, axis=0), jnp.sum(pre_norm * pre_norm, axis=0)), "bngroup"
    )
    centre = first_sum / number
    spread = jnp.maximum(second_sum / number - centre * centre, 0.0)
    inverse = lax.rsqrt(spread + EPS)
    scaled = (pre_norm - centre) * inverse
    return (scaled, inverse, norm_gain * scaled + norm_shift)


def norm_back(upstream, scaled, inverse, norm_gain, group_size):
    shift_sum, gain_sum = lax.psum(
        (jnp.sum(upstream, axis=0), jnp.sum(upstream * scaled, axis=0)), "bngroup"
    )
    number = upstream.shape[0] * group_size
    result = norm_gain * inverse * (upstream - shift_sum / number - scaled * gain_sum / number)
    return (result.astype(jnp.bfloat16), shift_sum, gain_sum)


def unfold(field):
    length = field.shape[1]
    padded = jnp.pad(field, ((0, 0), (1, 1), (1, 1), (0, 0)))
    windows = [
        padded[:, row_tap : row_tap + length, col_tap : col_tap + length, :]
        for row_tap in range(3)
        for col_tap in range(3)
    ]
    return jnp.concatenate(windows, axis=-1).reshape(-1, 9 * field.shape[3])


def fold_back(columns, images_count, length, channels):
    shaped = columns.reshape(images_count, length, length, 9, channels)
    summed = jnp.zeros((images_count, length + 2, length + 2, channels), jnp.float32)
    for row_tap in range(3):
        for col_tap in range(3):
            summed = summed + jnp.pad(
                shaped[:, :, :, 3 * row_tap + col_tap, :],
                ((0, 0), (row_tap, 2 - row_tap), (col_tap, 2 - col_tap), (0, 0)),
            )
    return summed[:, 1 : length + 1, 1 : length + 1, :].reshape(-1, channels)


def per_device(images, cotangent, w_reduce, w_spatial, w_expand, norm_gain, norm_shift):
    group_size = lax.axis_size("bngroup")
    images_total = images.shape[0] * group_size * lax.axis_size("rep")
    images_count = images.shape[0]
    length = images.shape[1]
    wide_ch = images.shape[3]
    mid_ch = w_reduce.shape[1]
    flat_in = images.reshape(-1, wide_ch)
    gain_one, gain_two, gain_three = (
        norm_gain[:mid_ch],
        norm_gain[mid_ch : 2 * mid_ch],
        norm_gain[2 * mid_ch :],
    )
    shift_one, shift_two, shift_three = (
        norm_shift[:mid_ch],
        norm_shift[mid_ch : 2 * mid_ch],
        norm_shift[2 * mid_ch :],
    )
    scaled_one, inverse_one, normed_one = normalize(
        matmul(flat_in, w_reduce), gain_one, shift_one, group_size
    )
    hidden_one = jax.nn.silu(normed_one).astype(jnp.bfloat16)
    patches = unfold(hidden_one.reshape(images_count, length, length, mid_ch))
    scaled_two, inverse_two, normed_two = normalize(
        matmul(patches, w_spatial), gain_two, shift_two, group_size
    )
    hidden_two = jax.nn.silu(normed_two).astype(jnp.bfloat16)
    scaled_three, inverse_three, normed_three = normalize(
        contract(hidden_two, w_expand, 1, 1), gain_three, shift_three, group_size
    )
    summed_in = normed_three + flat_in.astype(jnp.float32)
    output = jax.nn.silu(summed_in).astype(jnp.bfloat16)
    upstream = cotangent.reshape(-1, wide_ch).astype(jnp.float32) * slope(summed_in)
    grad_three, shift_sum_three, gain_sum_three = norm_back(
        upstream, scaled_three, inverse_three, gain_three, group_size
    )
    back_two = matmul(grad_three, w_expand) * slope(normed_two)
    grad_two, shift_sum_two, gain_sum_two = norm_back(
        back_two, scaled_two, inverse_two, gain_two, group_size
    )
    back_one = fold_back(contract(grad_two, w_spatial, 1, 1), images_count, length, mid_ch) * slope(
        normed_one
    )
    grad_one, shift_sum_one, gain_sum_one = norm_back(
        back_one, scaled_one, inverse_one, gain_one, group_size
    )
    in_grad = (upstream + contract(grad_one, w_reduce, 1, 1)).astype(jnp.bfloat16)
    local_grads = jnp.concatenate(
        [
            contract(flat_in, grad_one, 0, 0),
            contract(patches, grad_two, 0, 0),
            contract(grad_three, hidden_two, 0, 0),
        ],
        axis=0,
    )
    partial_grads = lax.psum_scatter(local_grads, "rep", scatter_dimension=1, tiled=True)
    summed_grads = lax.psum_scatter(partial_grads, "bngroup", scatter_dimension=0, tiled=True)
    group_norms = jnp.stack(
        [
            jnp.concatenate([gain_sum_one, gain_sum_two, gain_sum_three]),
            jnp.concatenate([shift_sum_one, shift_sum_two, shift_sum_three]),
        ]
    )
    norm_summed = lax.psum(group_norms, "rep")
    return (
        output.reshape(images.shape),
        in_grad.reshape(images.shape),
        summed_grads / images_total,
        norm_summed / images_total,
    )


def solution(mesh):
    in_specs = (
        P(("bngroup", "rep"), None, None, None),
        P(("bngroup", "rep"), None, None, None),
        P(),
        P(),
        P(),
        P(),
        P(),
    )
    out_specs = (
        P(("bngroup", "rep"), None, None, None),
        P(("bngroup", "rep"), None, None, None),
        P("bngroup", "rep"),
        P(),
    )
    return jax.shard_map(
        per_device, mesh=mesh, in_specs=in_specs, out_specs=out_specs, check_vma=False
    )
```

profile of v0, /device:TPU:0, one launch (start us, length us, event | category | flops | bytes accessed | tf_op | source)
XLA Modules:
  0.0 499.4 jit_solution(15517968195492733898)
XLA Ops:
  7.2 0.8 fusion.12
  8.1 4.2 reshape.61
  12.3 3.8 fusion.10
  16.1 13.5 %all-reduce.15 = (f32[512]{0:T(512)S(1)}, f32[512]{0:T(512)S(1)}) all-reduce(f32[512]{0:T(512)S(1)} %get-tuple-element.27, f32[512]{0:T(512)S(1)} %get-tuple-element.26), channel_id=1, replica_groups=mesh['bngroup'=4,'rep'=8] {'bngroup'}, use_global_device_ids=true, to_apply=%region_3.0 | all-reduce | flops 1024 | bytes 8192 | tf_op jit(solution)/shard_map/psum | solution.py:26
  29.6 1.2 multiply_convert_fusion.5
  30.8 2.0 reshape.62
  32.8 5.9 %pad_slice_fusion = (bf16[12,7,7,512]{3,2,1,0:T(8,128)(2,1)}, bf16[12,7,7,512]{3,2,1,0:T(8,128)(2,1)}, bf16[12,7,7,512]{3,2,1,0:T(8,128)(2,1)}, bf16[12,7,7,512]...) fusion(bf16[12,7,7,512]{3,2,1,0:T(8,128)(2,1)} %reshape.62), kind=kLoop, calls=%fused_computation.10 | loop fusion | bytes 5419008 | tf_op jit(solution)/shard_map/slice | solution.py:49
  38.8 2.1 concatenate.29
  40.8 2.0 constant_dynamic-update-slice_fusion.8
  42.8 2.1 concatenate.30
  44.8 2.1 concatenate.31
  46.9 2.1 concatenate.32
  49.1 2.1 constant_dynamic-update-slice_fusion.7
  51.2 0.9 constant_dynamic-update-slice_fusion.6
  52.0 0.9 constant_dynamic-update-slice_fusion.5
  53.0 1.3 constant_dynamic-update-slice_fusion.4
  54.2 2.1 concatenate.33
  56.3 2.1 concatenate.34
  58.4 2.1 concatenate.35
  60.5 2.1 concatenate.36
  62.5 4.6 reshape.67
  67.2 2.1 constant_dynamic-update-slice_fusion.3
  69.2 0.9 constant_dynamic-update-slice_fusion.2
  70.1 0.9 constant_dynamic-update-slice_fusion.1
  71.0 0.9 constant_dynamic-update-slice_fusion
  71.9 7.9 %fusion.9 = (f32[512]{0:T(512)S(1)}, f32[512]{0:T(512)S(1)}, f32[588,512]{1,0:T(8,128)}) fusion(bf16[588,4608]{1,0:T(8,128)(2,1)} %constant_dynamic-update-slice_fusion, bf16[4608,512]{1,0:T(8,128)(2,1)} %param.10), kind=kOutput, calls=%fused_computation.83 | convolution fusion | flops 2775434240 | bytes 11345920 | tf_op jit(solution)/shard_map/dot_general | solution.py:10
  79.8 8.3 %all-reduce.14 = (f32[512]{0:T(512)S(1)}, f32[512]{0:T(512)S(1)}) all-reduce(f32[512]{0:T(512)S(1)} %get-tuple-element.25, f32[512]{0:T(512)S(1)} %get-tuple-element.24), channel_id=1, replica_groups=mesh['bngroup'=4,'rep'=8] {'bngroup'}, use_global_device_ids=true, to_apply=%region_7.8 | all-reduce | flops 1024 | bytes 8192 | tf_op jit(solution)/shard_map/psum | solution.py:26
  88.2 5.1 %fusion.6 = (f32[2048]{0:T(1024)S(1)}, f32[2048]{0:T(1024)S(1)}, f32[588,2048]{1,0:T(8,128)}) fusion(bf16[2048,512]{1,0:T(8,128)(2,1)S(1)} %copy-done, f32[588,512]{1,0:T(8,128)} %get-tuple-element.74, f32[512]{0:T(512)S(1)} %get-tuple-element.66, f32[512]{0:T(512)S(1)} %get-tuple-element.69, f32[512]{0:T(512)S(1)} %get-tuple-element.70, ...), kind=kOutput, calls=%fused_computation.80 | convolution fusion | flops 1239443456 | bytes 8142848 | tf_op jit(solution)/shard_map/dot_general | solution.py:14
  93.3 17.4 %all-reduce.13 = (f32[2048]{0:T(1024)S(1)}, f32[2048]{0:T(1024)S(1)}) all-reduce(f32[2048]{0:T(1024)S(1)} %get-tuple-element.19, f32[2048]{0:T(1024)S(1)} %get-tuple-element.18), channel_id=1, replica_groups=mesh['bngroup'=4,'rep'=8] {'bngroup'}, use_global_device_ids=true, to_apply=%region_11.12 | all-reduce | flops 4096 | bytes 32768 | tf_op jit(solution)/shard_map/psum | solution.py:26
  110.7 7.9 %fusion.5 = (f32[2048]{0:T(1024)S(1)}, f32[2048]{0:T(1024)S(1)}, f32[588,2048]{1,0:T(8,128)}, bf16[588,2048]{1,0:T(8,128)(2,1)}) fusion(f32[2048]{0:T(1024)S(1)} %get-tuple-element.61, f32[588,2048]{1,0:T(8,128)} %get-tuple-element.75, f32[2048]{0:T(1024)S(1)} %get-tuple-element.68, f32[588,2048]{1,0:T(8,128)} %reshape.67, bf16[588,2048]{1,0:T(8,128)(2,1)} %reshape.61, ...), kind=kLoop, calls=%fused_computation.79 | loop fusion | flops 22876160 | bytes 19316736 | tf_op jit(solution)/shard_map/reduce_sum | solution.py:38
  118.6 15.7 %all-reduce.12 = (f32[2048]{0:T(1024)S(1)}, f32[2048]{0:T(1024)S(1)}) all-reduce(f32[2048]{0:T(1024)S(1)} %get-tuple-element.17, f32[2048]{0:T(1024)S(1)} %get-tuple-element.16), channel_id=1, replica_groups=mesh['bngroup'=4,'rep'=8] {'bngroup'}, use_global_device_ids=true, to_apply=%region_15.16 | all-reduce | flops 4096 | bytes 32768 | tf_op jit(solution)/shard_map/psum | solution.py:37
  134.3 5.2 %multiply_convert_fusion = bf16[588,2048]{1,0:T(8,128)(2,1)S(1)} fusion(f32[588,2048]{1,0:T(8,128)} %get-tuple-element.41, f32[588,2048]{1,0:T(8,128)} %get-tuple-element.75, f32[2048]{0:T(1024)S(1)} %get-tuple-element.32, f32[2048]{0:T(1024)S(1)} %broadcast_multiply_fusion.2, f32[2048]{0:T(1024)S(1)} %get-tuple-element.60, f32[2048]{0:T(1024)S(1)} %get-tuple-element.61, ...), kind=kLoop, calls=%fused_computation.2 | loop fusion | flops 9633792 | bytes 12083200 | tf_op jit(solution)/shard_map/convert_element_type | solution.py:42
  139.6 2.9 fusion.8
  142.5 9.1 %all-reduce.11 = (f32[512]{0:T(512)S(1)}, f32[512]{0:T(512)S(1)}) all-reduce(f32[512]{0:T(512)S(1)} %get-tuple-element.23, f32[512]{0:T(512)S(1)} %get-tuple-element.22), channel_id=1, replica_groups=mesh['bngroup'=4,'rep'=8] {'bngroup'}, use_global_device_ids=true, to_apply=%region_19.20 | all-reduce | flops 1024 | bytes 8192 | tf_op jit(solution)/shard_map/psum | solution.py:37
  151.6 2.1 multiply_convert_fusion.3
  153.7 8.1 %fusion.13 = f32[588,4608]{1,0:T(8,128)} fusion(bf16[588,512]{1,0:T(8,128)(2,1)S(1)} %multiply_convert_fusion.3, bf16[4608,512]{1,0:T(8,128)(2,1)} %param.10), kind=kOutput, calls=%fused_computation.87 | convolution fusion | flops 2774532096 | bytes 16158720 | tf_op jit(solution)/shard_map/dot_general | solution.py:14
  161.9 6.3 %fusion.14 = f32[4608,512]{1,0:T(8,128)} fusion(bf16[588,4608]{1,0:T(8,128)(2,1)S(1)} %bitcast.61, bf16[588,512]{1,0:T(8,128)(2,1)S(1)} %multiply_convert_fusion.3), kind=kOutput, calls=%fused_computation.88 | convolution fusion | flops 2774532096 | bytes 15458304 | tf_op jit(solution)/shard_map/dot_general | solution.py:14
  168.2 4.1 fusion.3
  172.2 14.0 %reshape.64 = f32[12,7,7,9,512]{4,3,2,1,0:T(8,128)} reshape(f32[588,4608]{1,0:T(8,128)} %fusion.13) | data formatting | bytes 21676032 | tf_op jit(solution)/shard_map/reshape | solution.py:57
  186.2 32.4 %fusion.11 = (f32[12,7,7,1,512]{4,3,2,1,0:T(1,128)}, f32[12,7,7,1,512]{4,3,2,1,0:T(1,128)}, f32[12,7,7,1,512]{4,3,2,1,0:T(1,128)}, f32[12,7,7,1,512]{4,3,2,1,0:T...) fusion(f32[12,7,7,9,512]{4,3,2,1,0:T(8,128)} %reshape.64), kind=kLoop, calls=%fused_computation.85 | loop fusion | bytes 21676032 | tf_op jit(solution)/shard_map/slice | solution.py:62
  218.6 1.6 copy.67
  220.5 1.0 copy-done.8
  222.2 0.9 copy-done.6
  223.8 0.9 copy-done.4
  225.7 0.8 pad_add_fusion
  226.5 1.1 pad_add_fusion.1
  227.7 1.2 reshape.65
  228.9 1.9 fusion.7
  230.8 9.6 %all-reduce.10 = (f32[512]{0:T(512)S(1)}, f32[512]{0:T(512)S(1)}) all-reduce(f32[512]{0:T(512)S(1)} %get-tuple-element.21, f32[512]{0:T(512)S(1)} %get-tuple-element.20), channel_id=1, replica_groups=mesh['bngroup'=4,'rep'=8] {'bngroup'}, use_global_device_ids=true, to_apply=%region_23.24 | all-reduce | flops 1024 | bytes 8192 | tf_op jit(solution)/shard_map/psum | solution.py:37
  240.8 1.4 copy-done.2
  242.1 3.9 convolution_bitcast_fusion
  246.0 5.3 %copy.40 = f32[2048,512]{1,0:T(8,128)} copy(f32[2048,512]{0,1:T(8,128)} %convolution_bitcast_fusion) | data formatting | bytes 8388608 | tf_op jit(solution)/shard_map/dot_general | solution.py:14
  251.3 14.6 %pad_maximum_fusion = f32[8704,512]{1,0:T(8,128)} fusion(f32[2048,512]{1,0:T(8,128)} %fusion.3, f32[4608,512]{1,0:T(8,128)} %fusion.14, f32[2048,512]{1,0:T(8,128)} %copy.40), kind=kLoop, calls=%fused_computation | loop fusion | flops 8912896 | bytes 35651584 | tf_op jit(solution)/shard_map/concatenate | solution.py:115
  266.0 18.1 %copy.42 = f32[8704,512]{0,1:T(8,128)} copy(f32[8704,512]{1,0:T(8,128)} %pad_maximum_fusion) | data formatting | bytes 35651584
  284.1 119.7 %reduce-scatter.7.cloned.1.call-done = f32[64,8704]{1,0:T(8,128)} async-done(((f32[512,8704]{1,0:T(8,128)}), f32[64,8704]{1,0:T(8,128)}) %reduce-scatter.7.cloned.1.call-update) | async-done | bytes 2228240
  403.8 4.8 copy.43
  408.7 5.9 %add_convert_fusion = bf16[588,2048]{1,0:T(8,128)(2,1)} fusion(f32[588,2048]{1,0:T(8,128)} %get-tuple-element.41, bf16[588,512]{1,0:T(8,128)(2,1)S(1)} %multiply_convert_fusion.2, bf16[2048,512]{1,0:T(8,128)(2,1)} %param.9), kind=kOutput, calls=%fused_computation.1 | convolution fusion | flops 1235533824 | bytes 9924608 | tf_op jit(solution)/shard_map/dot_general | solution.py:14
  414.6 4.4 reshape.66
  419.0 4.2 reshape.63
  423.2 24.3 %psum.103 = f32[2,3072]{1,0:T(2,128)S(1)} all-reduce(f32[2,3072]{1,0:T(2,128)S(1)} %pad_maximum_fusion.1), channel_id=1, replica_groups=mesh['bngroup'=4,'rep'=8] {'rep'}, use_global_device_ids=true, to_apply=%region_26.27 | all-reduce | flops 6144 | bytes 49152 | tf_op jit(solution)/shard_map/psum | solution.py:131
  447.6 0.6 broadcast_multiply_fusion.1
  448.2 41.7 %reduce-scatter.5.cloned.1.call-done = f32[2176,64]{1,0:T(8,128)} async-done(((f32[8704,64]{1,0:T(8,128)}), f32[2176,64]{1,0:T(8,128)}) %reduce-scatter.5.cloned.1.call-update) | async-done | bytes 557072 | tf_op jit(solution)/shard_map/reduce_scatter | solution.py:124
  489.9 1.5 broadcast_multiply_fusion
  491.4 1.2 copy.41
  (65 shorter events, 3.2 us)
Async XLA Ops:
  7.2 81.0 %copy-start = (bf16[2048,512]{1,0:T(8,128)(2,1)S(1)}, bf16[2048,512]{1,0:T(8,128)(2,1)}, u32[]{:S(2)}) copy-start(bf16[2048,512]{1,0:T(8,128)(2,1)} %param.11) | copy-start | bytes 6291460
  7.2 396.6 %reduce-scatter.7.cloned.1.call-start = ((), (), s32[]{:S(2)}) async-start(), calls=%async_computation.3 | async-start | bytes 20054016
  8.1 4.2 copy-start.19
  49.1 2.1 copy-start.14
  49.1 3.0 copy-start.13
  67.2 2.1 copy-start.12
  67.2 2.9 copy-start.10
  69.2 1.8 copy-start.11
  88.2 22.5 %slice-start.2 = ((f32[3072]{0:T(1024)}), f32[2048]{0:T(1024)S(1)}, s32[]{:S(2)}) async-start(f32[3072]{0:T(1024)} %param.13), calls=%async_computation.6 | async-start | bytes 16384 | tf_op jit(solution)/shard_map/slice | solution.py:84
  134.3 5.2 %copy-start.17 = (f32[588,512]{1,0:T(8,128)S(1)}, f32[588,512]{1,0:T(8,128)}, u32[]{:S(2)}) copy-start(f32[588,512]{1,0:T(8,128)} %get-tuple-element.74) | copy-start | bytes 3612676
  139.6 2.9 copy-start.15
  151.6 10.3 %slice-start = ((s8[5455872]{0:T(1024)(128)(4,1)}), s8[4194304]{0:T(1024)(128)(4,1)S(1)}, s32[]{:S(2)}) async-start(s8[5455872]{0:T(1024)(128)(4,1)} %bitcast.60), calls=%async_computation.4 | async-start | bytes 8388608
  153.7 8.1 %slice-start.1 = ((s8[5455872]{0:T(1024)(128)(4,1)}), s8[1261568]{0:T(1024)(128)(4,1)S(1)}, s32[]{:S(2)}) async-start(s8[5455872]{0:T(1024)(128)(4,1)} %bitcast.60), calls=%async_computation.5 | async-start | bytes 2523136
  161.8 6.3 %copy-start.16 = (bf16[588,2048]{1,0:T(8,128)(2,1)S(1)}, bf16[588,2048]{1,0:T(8,128)(2,1)}, u32[]{:S(2)}) copy-start(bf16[588,2048]{1,0:T(8,128)(2,1)} %copy-done.15) | copy-start | bytes 7225348
  161.8 6.3 %copy-start.18 = (f32[588,512]{1,0:T(8,128)S(1)}, f32[588,512]{1,0:T(8,128)}, u32[]{:S(2)}) copy-start(f32[588,512]{1,0:T(8,128)} %get-tuple-element.74) | copy-start | bytes 3612676
  218.6 1.6 copy-start.9
  220.2 1.3 copy-start.8
  220.5 1.4 copy-start.7
  221.8 1.3 copy-start.6
  222.2 1.4 copy-start.5
  223.3 1.3 copy-start.4
  223.8 1.4 copy-start.3
  240.4 1.7 copy-start.2
  284.1 205.8 %reduce-scatter.5.cloned.1.call-start = ((), (), s32[]{:S(2)}) async-start(), calls=%async_computation.2 | async-start | bytes 5570560 | tf_op jit(solution)/shard_map/reduce_scatter | solution.py:124
  489.9 2.7 copy-start.1
Sparse Core Ops, SparseCore 0:
  284.2 119.5 reduce-scatter.6
  408.8 81.0 reduce-scatter.4
where the time goes:
time: 501 us; the launch traced here: 499 us
  waiting for transfers between devices  161 us (32%)
  local copies, waits for them, and re-layouts  139 us (28%)
  blocking collectives  98 us (20%)
  matrix products  47.9 us (10%)
  other arithmetic  38.8 us (8%)
  between operations  14.3 us (3%)
    unnamed x3, waiting for transfers between devices  120 us
    unnamed x63, local copies, waits for them, and re-layouts  42.1 us
    reduce_scatter x1, waiting for transfers between devices, per_device(): lax.psum_scatter(partial_grads, 'bngroup', scatter_dimension=0, tiled=True)  41.7 us
    psum x3, blocking collectives, normalize(): lax.psum((jnp.sum(pre_norm, axis=0), jnp.sum(pre_norm * pre_norm, axis=0)...  39.2 us
    psum x3, blocking collectives, norm_back(): lax.psum((jnp.sum(upstream, axis=0), jnp.sum(upstream * scaled, axis=0)),...  34.5 us
    dot_general x6, matrix products, contract(): lax.dot_general(left, right, (((left_dim,), (right_dim,)), ((), ())), pre...  33.3 us
    slice x1, local copies, waits for them, and re-layouts, fold_back(): shaped[:, :, :, 3 * row_tap + col_tap, :]  32.4 us
    psum x1, blocking collectives, per_device(): norm_summed = lax.psum(group_norms, 'rep')  24.3 us
  transfers between devices with their start and end apart: 2, of which 2 were waited for; matrix products, arithmetic and copies ran while one was open for 3% of the time, Pallas kernels for 0%

commit v1 on v0

--- a/solution.py
+++ b/solution.py
@@ -1,7 +1,13 @@
+import functools
+
 import jax
 import jax.numpy as jnp
 from jax import lax
+from jax.experimental import pallas as pl
+from jax.experimental.pallas import tpu as pltpu
 from jax.sharding import PartitionSpec as P
+
+MESH = pl.DeviceIdType.MESH
 
 EPS = 0.25
 
@@ -16,16 +22,272 @@
     )
 
 
+def exchange_kernel(axis, size, value_ref, total_ref, slots, send_sem, recv_sem):
+    me = lax.axis_index(axis)
+    barrier = pltpu.get_barrier_semaphore()
+    for step in range(1, size):
+        peer = lax.rem(me + step, size)
+        pl.semaphore_signal(barrier, inc=1, device_id={axis: peer}, device_id_type=MESH)
+    pl.semaphore_wait(barrier, size - 1)
+    copies = []
+    for step in range(1, size):
+        peer = lax.rem(me + step, size)
+        copy = pltpu.make_async_remote_copy(
+            src_ref=value_ref,
+            dst_ref=slots.at[me],
+            send_sem=send_sem.at[step],
+            recv_sem=recv_sem.at[step],
+            device_id={axis: peer},
+            device_id_type=MESH,
+        )
+        copy.start()
+        copies.append(copy)
+    slots[me] = value_ref[...]
+    for copy in copies:
+        copy.wait()
+    total = slots[0]
+    for member in range(1, size):
+        total = total + slots[member]
+    total_ref[...] = total
+
+
+def exchange_sum(value, axis, ident):
+    size = lax.axis_size(axis)
+    return pl.pallas_call(
+        functools.partial(exchange_kernel, axis, size),
+        out_shape=jax.ShapeDtypeStruct(value.shape, value.dtype),
+        in_specs=[pl.BlockSpec(memory_space=pltpu.VMEM)],
+        out_specs=pl.BlockSpec(memory_space=pltpu.VMEM),
+        scratch_shapes=[
+            pltpu.VMEM((size,) + value.shape, value.dtype),
+            pltpu.SemaphoreType.DMA((size,)),
+            pltpu.SemaphoreType.DMA((size,)),
+        ],
+        compiler_params=pltpu.CompilerParams(collective_id=ident, has_side_effects=True),
+        name="exchange_" + str(ident),
+    )(value)
+
+
+def weight_kernel(starts, grad_one, flat_in, grad_two, patches, hidden_two, grad_three, out_ref):
+    at = pl.program_id(0)
+
+    @pl.when(at < starts[0])
+    def _():
+        out_ref[...] = contract(grad_one[...], flat_in[...], 0, 0)
+
+    @pl.when(jnp.logical_and(at >= starts[0], at < starts[1]))
+    def _():
+        out_ref[...] = contract(grad_two[...], patches[...], 0, 0)
+
+    @pl.when(at >= starts[1])
+    def _():
+        out_ref[...] = contract(hidden_two[...], grad_three[...], 0, 0)
+
+
+def weight_products(grad_one, flat_in, grad_two, patches, hidden_two, grad_three):
+    rows, mid = grad_one.shape
+    counts = [array.shape[1] // mid for array in (flat_in, patches, grad_three)]
+    starts = (counts[0], counts[0] + counts[1])
+    whole = pl.BlockSpec((rows, mid), lambda at: (0, 0))
+
+    def columns(first, count):
+        return pl.BlockSpec((rows, mid), lambda at: (0, jnp.clip(at - first, 0, count - 1)))
+
+    return pl.pallas_call(
+        functools.partial(weight_kernel, starts),
+        grid=(sum(counts),),
+        out_shape=jax.ShapeDtypeStruct((mid, sum(counts) * mid), jnp.float32),
+        in_specs=[
+            whole,
+            columns(0, counts[0]),
+            whole,
+            columns(starts[0], counts[1]),
+            whole,
+            columns(starts[1], counts[2]),
+        ],
+        out_specs=pl.BlockSpec((mid, mid), lambda at: (0, at)),
+        name="weight_products",
+    )(grad_one, flat_in, grad_two, patches, hidden_two, grad_three)
+
+
+def scatter_plan(n_group, n_rep, rows):
+    bits = [("rep", at) for at in range(n_rep.bit_length() - 1)]
+    bits += [("bngroup", at) for at in range(n_group.bit_length() - 1)]
+    rest = len(bits) - 1
+    near = list(range(rest))
+    rep_rest = n_rep.bit_length() - 2
+    orders = [
+        near,
+        near[1:rep_rest] + near[rep_rest:] + near[:1],
+        near[rep_rest:] + near[:rep_rest],
+    ]
+    tiles = rows // 8
+    sizes = [(tiles + 2) // 3, (tiles + 1) // 3, tiles // 3]
+    streams, begin = [], 0
+    for order, size in zip(orders, sizes):
+        if size:
+            streams.append((begin * 8, size * 8, order))
+        begin += size
+    return bits, streams
+
+
+def scatter_kernel(n_group, n_rep, scale, grads, out_ref, own, got, load_sem, send_sem, recv_sem):
+    rows, cols = out_ref.shape
+    bits, streams = scatter_plan(n_group, n_rep, rows)
+    rest = bits[1:]
+    place = {"rep": lax.axis_index("rep"), "bngroup": lax.axis_index("bngroup")}
+
+    def flipped(value, at):
+        bit = lax.rem(value // (1 << at), 2)
+        return value + (1 - 2 * bit) * (1 << at)
+
+    def partner(axis, at):
+        return {axis: flipped(place[axis], at)}
+
+    barrier = pltpu.get_barrier_semaphore()
+    for axis, at in bits:
+        pl.semaphore_signal(barrier, inc=1, device_id=partner(axis, at), device_id_type=MESH)
+
+    def source(relative, other, begin, size):
+        spot = dict(place)
+        for index, (axis, at) in enumerate(rest):
+            if relative >> index & 1:
+                spot[axis] = flipped(spot[axis], at)
+        if other:
+            spot["rep"] = flipped(spot["rep"], 0)
+        first = pl.multiple_of(spot["rep"] * rows + begin, 8)
+        if len(grads.shape) == 3:
+            return grads.at[spot["bngroup"], pl.ds(first, size), :]
+        return grads.at[pl.ds(first, size), pl.ds(pl.multiple_of(spot["bngroup"] * cols, 128), cols)]
+
+    count = 1 << len(rest)
+    slot_of, slots = {}, count
+    for number, (begin, size, order) in enumerate(streams):
+        used = count
+        active = list(range(count))
+        for stage, bit in enumerate(order):
+            active = [relative for relative in active if not relative >> bit & 1]
+            for relative in active:
+                slot_of[number, stage, relative] = used
+                used += 1
+
+    def first_order(order):
+        ranks = sorted(range(count), key=lambda rel: tuple(-(rel >> bit & 1) for bit in order))
+        return ranks
+
+    loads = {}
+    for number, (begin, size, order) in enumerate(streams):
+        for relative in range(count):
+            copy = pltpu.make_async_copy(
+                source(relative, False, begin, size),
+                own.at[relative, pl.ds(begin, size), :],
+                load_sem.at[number, relative],
+            )
+            loads[number, relative] = copy
+    for relative in range(count):
+        for number, (begin, size, order) in enumerate(streams):
+            loads[number, first_order(order)[relative]].start()
+    pl.semaphore_wait(barrier, len(bits))
+    sent = []
+    arrivals = {}
+    for relative in range(count):
+        for number, (begin, size, order) in enumerate(streams):
+            which = first_order(order)[relative]
+            copy = pltpu.make_async_remote_copy(
+                src_ref=source(which, True, begin, size),
+                dst_ref=got.at[which, pl.ds(begin, size), :],
+                send_sem=send_sem.at[number, which],
+                recv_sem=recv_sem.at[number, which],
+                device_id=partner(*bits[0]),
+                device_id_type=MESH,
+            )
+            copy.start()
+            sent.append(copy)
+            arrivals[number, -1, which] = copy
+
+    def onward(number, stage, relative):
+        begin, size, order = streams[number]
+        bit = order[stage]
+        slot = slot_of[number, stage, relative & ~(1 << bit)]
+        copy = pltpu.make_async_remote_copy(
+            src_ref=own.at[relative, pl.ds(begin, size), :],
+            dst_ref=got.at[slot, pl.ds(begin, size), :],
+            send_sem=send_sem.at[number, slot],
+            recv_sem=recv_sem.at[number, slot],
+            device_id=partner(*rest[bit]),
+            device_id_type=MESH,
+        )
+        copy.start()
+        sent.append(copy)
+        arrivals[number, stage, relative & ~(1 << bit)] = copy
+
+    pending = []
+    for stage in range(-1, len(rest)):
+        active = []
+        for number, (begin, size, order) in enumerate(streams):
+            done = 0
+            for bit in order[: stage + 1]:
+                done |= 1 << bit
+            active.append([rel for rel in first_order(order) if not rel & done])
+        for position in range(len(active[0])):
+            for number, (begin, size, order) in enumerate(streams):
+                relative = active[number][position]
+                slot = relative if stage < 0 else slot_of[number, stage, relative]
+                if stage < 0:
+                    loads[number, relative].wait()
+                arrivals[number, stage, relative].wait_recv()
+                window = pl.ds(begin, size)
+                total = own[relative, window, :] + got[slot, window, :]
+                if stage == len(rest) - 1:
+                    out_ref[window, :] = total * scale
+                else:
+                    own[relative, window, :] = total
+                while pending:
+                    onward(*pending.pop(0))
+                if stage + 1 < len(rest) and relative >> order[stage + 1] & 1:
+                    pending.append((number, stage + 1, relative))
+        while pending:
+            onward(*pending.pop(0))
+    for copy in sent:
+        copy.wait_send()
+
+
+def scatter_sum(grads, images_total, ident):
+    n_group, n_rep = lax.axis_size("bngroup"), lax.axis_size("rep")
+    rows, cols = grads.shape[0] // n_rep, grads.shape[1] // n_group
+    if cols % 128:
+        grads = grads.reshape(grads.shape[0], n_group, cols).transpose(1, 0, 2)
+    bits, streams = scatter_plan(n_group, n_rep, rows)
+    count = 1 << (len(bits) - 1)
+    held = 2 * count - 1
+    return pl.pallas_call(
+        functools.partial(scatter_kernel, n_group, n_rep, 1.0 / images_total),
+        out_shape=jax.ShapeDtypeStruct((rows, cols), jnp.float32),
+        in_specs=[pl.BlockSpec(memory_space=pl.ANY)],
+        out_specs=pl.BlockSpec(memory_space=pltpu.VMEM),
+        scratch_shapes=[
+            pltpu.VMEM((count, rows, cols), jnp.float32),
+            pltpu.VMEM((held, rows, cols), jnp.float32),
+            pltpu.SemaphoreType.DMA((len(streams), count)),
+            pltpu.SemaphoreType.DMA((len(streams), held)),
+            pltpu.SemaphoreType.DMA((len(streams), held)),
+        ],
+        compiler_params=pltpu.CompilerParams(
+            collective_id=ident, has_side_effects=True, vmem_limit_bytes=60 * 1024 * 1024
+        ),
+        name="scatter_sum",
+    )(grads)
+
+
 def slope(value):
     sigma = jax.nn.sigmoid(value)
     return sigma * (1.0 + value * (1.0 - sigma))
 
 
-def normalize(pre_norm, norm_gain, norm_shift, group_size):
+def normalize(pre_norm, norm_gain, norm_shift, group_size, ident):
     number = pre_norm.shape[0] * group_size
-    first_sum, second_sum = lax.psum(
-        (jnp.sum(pre_norm, axis=0), jnp.sum(pre_norm * pre_norm, axis=0)), "bngroup"
-    )
+    sums = jnp.stack([jnp.sum(pre_norm, axis=0), jnp.sum(pre_norm * pre_norm, axis=0)])
+    first_sum, second_sum = exchange_sum(sums, "bngroup", ident)
     centre = first_sum / number
     spread = jnp.maximum(second_sum / number - centre * centre, 0.0)
     inverse = lax.rsqrt(spread + EPS)
@@ -33,10 +295,9 @@
     return (scaled, inverse, norm_gain * scaled + norm_shift)
 
 
-def norm_back(upstream, scaled, inverse, norm_gain, group_size):
-    shift_sum, gain_sum = lax.psum(
-        (jnp.sum(upstream, axis=0), jnp.sum(upstream * scaled, axis=0)), "bngroup"
-    )
+def norm_back(upstream, scaled, inverse, norm_gain, group_size, ident):
+    sums = jnp.stack([jnp.sum(upstream, axis=0), jnp.sum(upstream * scaled, axis=0)])
+    shift_sum, gain_sum = exchange_sum(sums, "bngroup", ident)
     number = upstream.shape[0] * group_size
     result = norm_gain * inverse * (upstream - shift_sum / number - scaled * gain_sum / number)
     return (result.astype(jnp.bfloat16), shift_sum, gain_sum)
@@ -84,55 +345,49 @@
         norm_shift[2 * mid_ch :],
     )
     scaled_one, inverse_one, normed_one = normalize(
-        matmul(flat_in, w_reduce), gain_one, shift_one, group_size
+        matmul(flat_in, w_reduce), gain_one, shift_one, group_size, 0
     )
     hidden_one = jax.nn.silu(normed_one).astype(jnp.bfloat16)
     patches = unfold(hidden_one.reshape(images_count, length, length, mid_ch))
     scaled_two, inverse_two, normed_two = normalize(
-        matmul(patches, w_spatial), gain_two, shift_two, group_size
+        matmul(patches, w_spatial), gain_two, shift_two, group_size, 1
     )
     hidden_two = jax.nn.silu(normed_two).astype(jnp.bfloat16)
     scaled_three, inverse_three, normed_three = normalize(
-        contract(hidden_two, w_expand, 1, 1), gain_three, shift_three, group_size
+        contract(hidden_two, w_expand, 1, 1), gain_three, shift_three, group_size, 2
     )
     summed_in = normed_three + flat_in.astype(jnp.float32)
     output = jax.nn.silu(summed_in).astype(jnp.bfloat16)
     upstream = cotangent.reshape(-1, wide_ch).astype(jnp.float32) * slope(summed_in)
     grad_three, shift_sum_three, gain_sum_three = norm_back(
-        upstream, scaled_three, inverse_three, gain_three, group_size
+        upstream, scaled_three, inverse_three, gain_three, group_size, 3
     )
     back_two = matmul(grad_three, w_expand) * slope(normed_two)
     grad_two, shift_sum_two, gain_sum_two = norm_back(
-        back_two, scaled_two, inverse_two, gain_two, group_size
+        back_two, scaled_two, inverse_two, gain_two, group_size, 4
     )
     back_one = fold_back(contract(grad_two, w_spatial, 1, 1), images_count, length, mid_ch) * slope(
         normed_one
     )
     grad_one, shift_sum_one, gain_sum_one = norm_back(
-        back_one, scaled_one, inverse_one, gain_one, group_size
+        back_one, scaled_one, inverse_one, gain_one, group_size, 5
     )
     in_grad = (upstream + contract(grad_one, w_reduce, 1, 1)).astype(jnp.bfloat16)
-    local_grads = jnp.concatenate(
-        [
-            contract(flat_in, grad_one, 0, 0),
-            contract(patches, grad_two, 0, 0),
-            contract(grad_three, hidden_two, 0, 0),
-        ],
-        axis=0,
-    )
-    partial_grads = lax.psum_scatter(local_grads, "rep", scatter_dimension=1, tiled=True)
-    summed_grads = lax.psum_scatter(partial_grads, "bngroup", scatter_dimension=0, tiled=True)
+    local_grads = weight_products(
+        grad_one, flat_in, grad_two, patches, hidden_two, grad_three
+    )
+    summed_grads = scatter_sum(local_grads, images_total, 7).T
     group_norms = jnp.stack(
         [
             jnp.concatenate([gain_sum_one, gain_sum_two, gain_sum_three]),
             jnp.concatenate([shift_sum_one, shift_sum_two, shift_sum_three]),
         ]
     )
-    norm_summed = lax.psum(group_norms, "rep")
+    norm_summed = exchange_sum(group_norms, "rep", 6)
     return (
         output.reshape(images.shape),
         in_grad.reshape(images.shape),
-        summed_grads / images_total,
+        summed_grads,
         norm_summed / images_total,
     )
 

time: 501 us -> 346 us (0.69)
  Pallas kernels: 0 us -> 162 us
  waiting for transfers between devices: 161 us -> 0 us
  blocking collectives: 98 us -> 0 us
  local copies, waits for them, and re-layouts: 139 us -> 112 us
  matrix products: 47.9 us -> 32.4 us
  between operations: 14.3 us -> 0.98 us
    pallas_call x0 -> x9, Pallas kernels: none -> 162 us  [the longest x1 90.3 us: scatter_sum(): pl.pallas_call(functools.partial(scatter_kernel, n_group, n_rep, 1.0 / im...]
    unnamed x3 -> x0, waiting for transfers between devices: 120 us -> none
    psum x7 -> x0, blocking collectives: 98 us -> none  [the longest x3 39.2 us: normalize(): lax.psum((jnp.sum(pre_norm, axis=0), jnp.sum(pre_norm * pre_norm, axis=0)...]
    reduce_scatter x1 -> x0, waiting for transfers between devices: 41.7 us -> none  [per_device(): lax.psum_scatter(partial_grads, 'bngroup', scatter_dimension=0, tiled=True)]
    unnamed x63 -> x41, local copies, waits for them, and re-layouts: 42.1 us -> 17.3 us
    dot_general x6 -> x3, matrix products: 33.3 us -> 17.8 us  [contract(): lax.dot_general(left, right, (((left_dim,), (right_dim,)), ((), ())), pre...]
    concatenate x1, other arithmetic: 14.6 us -> 0.01 us  [per_device(): jnp.concatenate([shift_sum_one, shift_sum_two, shift_sum_three])]
    another operation x0 -> x9, other arithmetic: none -> 5.98 us  [the longest x3 2.33 us: norm_back(): shift_sum, gain_sum = exchange_sum(sums, 'bngroup', ident)]
  transfers between devices with their start and end apart: 2 -> 0, of which waited for: 2 -> 0; matrix products, arithmetic and copies ran while one was open for 3% -> 0% of each run, Pallas kernels for 0% -> 0%
where the time goes in v1:
time: 346 us; the launch traced here: 344 us
  Pallas kernels  162 us (47%)
  local copies, waits for them, and re-layouts  112 us (32%)
  other arithmetic  36.9 us (11%)
  matrix products  32.4 us (9%)
    pallas_call x1, Pallas kernels, scatter_sum(): pl.pallas_call(functools.partial(scatter_kernel, n_group, n_rep, 1.0 / im...  90.3 us
    pallas_call x7, Pallas kernels, exchange_sum(): pl.pallas_call(functools.partial(exchange_kernel, axis, size), out_shape=...  51 us
    slice x1, local copies, waits for them, and re-layouts, fold_back(): shaped[:, :, :, 3 * row_tap + col_tap, :]  32 us
    pallas_call x1, Pallas kernels, weight_products(): pl.pallas_call(functools.partial(weight_kernel, starts), grid=(sum(counts...  20.1 us
    concatenate x9, local copies, waits for them, and re-layouts, unfold(): return jnp.concatenate(windows, axis=-1).reshape(-1, 9 * field.shape[3])  18.5 us
    dot_general x3, matrix products, contract(): lax.dot_general(left, right, (((left_dim,), (right_dim,)), ((), ())), pre...  17.8 us
    unnamed x41, local copies, waits for them, and re-layouts  17.3 us
    dot_general x3, matrix products, matmul(): return jnp.dot(left, right, preferred_element_type=jnp.float32)  14.6 us

profile of v1, /device:TPU:0, one launch (start us, length us, event | category | flops | bytes accessed | tf_op | source)
XLA Modules:
  0.0 343.5 jit_solution(15176745013693906889)
XLA Ops:
  0.6 4.4 %reshape.73.flat_in = bf16[588,2048]{1,0:T(8,128)(2,1)} reshape(bf16[12,7,7,2048]{3,2,1,0:T(8,128)(2,1)} %param.7) | data formatting | bytes 4816896 | tf_op jit(solution)/shard_map/reshape | solution.py:336
  5.0 3.8 %fusion.5 = (f32[512]{0:T(512)S(1)}, f32[512]{0:T(512)S(1)}, f32[588,512]{1,0:T(8,128)S(1)}) fusion(bf16[588,2048]{1,0:T(8,128)(2,1)} %reshape.73.flat_in, bf16[2048,512]{1,0:T(8,128)(2,1)} %param.9), kind=kOutput, calls=%fused_computation.85 | convolution fusion | flops 1234027520 | bytes 5713920 | tf_op jit(solution)/shard_map/dot_general | solution.py:16
  9.4 8.6 %exchange_0.1 = f32[2,512]{1,0:T(2,128)} custom-call(f32[2,512]{1,0:T(2,128)} %pad_maximum_fusion.5.value_ref), custom_call_target="tpu_custom_call" | custom-call | tf_op jit(solution)/shard_map/exchange_0/pallas_call | solution.py:56
  18.0 0.8 slice_multiply_fusion.2
  18.8 1.2 multiply_convert_fusion.5
  20.1 2.0 reshape.74
  22.1 5.5 %pad_slice_fusion = (bf16[12,7,7,512]{3,2,1,0:T(8,128)(2,1)}, bf16[12,7,7,512]{3,2,1,0:T(8,128)(2,1)}, bf16[12,7,7,512]{3,2,1,0:T(8,128)(2,1)}, bf16[12,7,7,512]...) fusion(bf16[12,7,7,512]{3,2,1,0:T(8,128)(2,1)} %reshape.74), kind=kLoop, calls=%fused_computation.9 | loop fusion | bytes 5419008 | tf_op jit(solution)/shard_map/slice | solution.py:310
  27.6 2.1 concatenate.26
  29.7 2.0 constant_dynamic-update-slice_fusion.8
  31.7 2.1 concatenate.27
  33.7 2.0 constant_dynamic-update-slice_fusion.7
  35.7 2.1 concatenate.28
  37.8 1.9 constant_dynamic-update-slice_fusion.6
  39.7 2.1 concatenate.29
  41.8 1.9 constant_dynamic-update-slice_fusion.5
  43.7 1.3 constant_dynamic-update-slice_fusion.4
  45.0 2.1 concatenate.30
  47.0 2.0 constant_dynamic-update-slice_fusion.3
  49.0 2.1 concatenate.31
  51.1 2.0 constant_dynamic-update-slice_fusion.2
  53.1 2.1 concatenate.32
  55.1 1.9 constant_dynamic-update-slice_fusion.1
  57.1 2.1 concatenate.33
  59.1 2.0 constant_dynamic-update-slice_fusion.patches
  61.2 8.0 %fusion.4 = (f32[512]{0:T(512)S(1)}, f32[512]{0:T(512)S(1)}, f32[588,512]{1,0:T(8,128)}) fusion(bf16[588,4608]{1,0:T(8,128)(2,1)} %constant_dynamic-update-slice_fusion.patches, bf16[4608,512]{1,0:T(8,128)(2,1)} %param.10), kind=kOutput, calls=%fused_computation.84 | convolution fusion | flops 2775434240 | bytes 11345920 | tf_op jit(solution)/shard_map/dot_general | solution.py:16
  69.8 6.8 %exchange_1.1 = f32[2,512]{1,0:T(2,128)} custom-call(f32[2,512]{1,0:T(2,128)} %pad_maximum_fusion.6.value_ref), custom_call_target="tpu_custom_call" | custom-call | tf_op jit(solution)/shard_map/exchange_1/pallas_call | solution.py:56
  76.6 0.8 slice_multiply_fusion.1
  77.4 1.7 multiply_convert_fusion.4.hidden_two
  79.1 3.6 %fusion.1 = (f32[2048]{0:T(1024)S(1)}, f32[2048]{0:T(1024)S(1)}, f32[588,2048]{1,0:T(8,128)}) fusion(bf16[588,512]{1,0:T(8,128)(2,1)S(1)} %multiply_convert_fusion.4.hidden_two, bf16[2048,512]{1,0:T(8,128)(2,1)S(1)} %copy-done), kind=kOutput, calls=%fused_computation.81 | convolution fusion | flops 1236733952 | bytes 7532544 | tf_op jit(solution)/shard_map/dot_general | solution.py:20
  82.7 0.6 pad_maximum_fusion.1.value_ref
  83.4 7.3 %exchange_2.1 = f32[2,2048]{1,0:T(2,128)} custom-call(f32[2,2048]{1,0:T(2,128)} %pad_maximum_fusion.1.value_ref), custom_call_target="tpu_custom_call" | custom-call | tf_op jit(solution)/shard_map/exchange_2/pallas_call | solution.py:56
  90.6 0.8 slice_multiply_fusion
  91.5 4.6 %reshape.79 = f32[588,2048]{1,0:T(8,128)} reshape(bf16[12,7,7,2048]{3,2,1,0:T(8,128)(2,1)} %param.8) | data formatting | bytes 7225344 | tf_op jit(solution)/shard_map/convert_element_type | solution.py:361
  96.1 8.0 %fusion = (f32[2048]{0:T(1024)S(1)}, f32[2048]{0:T(1024)S(1)}, f32[588,2048]{1,0:T(8,128)}, bf16[588,2048]{1,0:T(8,128)(2,1)}) fusion(f32[2048]{0:T(1024)S(1)} %bitcast.64, f32[588,2048]{1,0:T(8,128)} %get-tuple-element.60, f32[2048]{0:T(1024)S(1)} %bitcast.71, f32[588,2048]{1,0:T(8,128)} %reshape.79, bf16[588,2048]{1,0:T(8,128)(2,1)} %reshape.73.flat_in, ...), kind=kLoop, calls=%fused_computation.80 | loop fusion | flops 22876160 | bytes 19316736 | tf_op jit(solution)/shard_map/reduce_sum | solution.py:299
  104.1 0.6 pad_maximum_fusion.2.value_ref
  104.7 7.3 %exchange_3.1 = f32[2,2048]{1,0:T(2,128)} custom-call(f32[2,2048]{1,0:T(2,128)} %pad_maximum_fusion.2.value_ref), custom_call_target="tpu_custom_call" | custom-call | tf_op jit(solution)/shard_map/exchange_3/pallas_call | solution.py:56
  112.0 0.8 fusion.7
  112.8 5.2 %multiply_convert_fusion.grad_three = bf16[588,2048]{1,0:T(8,128)(2,1)S(1)} fusion(f32[588,2048]{1,0:T(8,128)} %get-tuple-element.17, f32[588,2048]{1,0:T(8,128)} %get-tuple-element.60, f32[2048]{0:T(1024)S(1)} %bitcast.73, f32[2048]{0:T(1024)S(1)} %bitcast.88, f32[2048]{0:T(1024)S(1)} %get-tuple-element.44, f32[2048]{0:T(1024)S(1)} %bitcast.65, ...), kind=kLoop, calls=%fused_computation.1 | loop fusion | flops 9633792 | bytes 12083200 | tf_op jit(solution)/shard_map/convert_element_type | solution.py:303
  118.1 2.9 fusion.3
  121.5 6.8 %exchange_4.1 = f32[2,512]{1,0:T(2,128)} custom-call(f32[2,512]{1,0:T(2,128)} %pad_maximum_fusion.7.value_ref), custom_call_target="tpu_custom_call" | custom-call | tf_op jit(solution)/shard_map/exchange_4/pallas_call | solution.py:56
  128.4 0.8 fusion.10
  129.1 2.0 multiply_convert_fusion.3.grad_two
  131.1 8.3 %fusion.11 = f32[588,4608]{1,0:T(8,128)} fusion(bf16[588,512]{1,0:T(8,128)(2,1)S(1)} %multiply_convert_fusion.3.grad_two, bf16[4608,512]{1,0:T(8,128)(2,1)} %param.10), kind=kOutput, calls=%fused_computation.91 | convolution fusion | flops 2774532096 | bytes 16158720 | tf_op jit(solution)/shard_map/dot_general | solution.py:20
  139.4 13.9 %reshape.76 = f32[12,7,7,9,512]{4,3,2,1,0:T(8,128)} reshape(f32[588,4608]{1,0:T(8,128)} %fusion.11) | data formatting | bytes 21676032 | tf_op jit(solution)/shard_map/reshape | solution.py:318
  153.3 32.0 %fusion.6 = (f32[12,7,7,1,512]{4,3,2,1,0:T(1,128)S(1)}, f32[12,7,7,1,512]{4,3,2,1,0:T(1,128)S(1)}, f32[12,7,7,1,512]{4,3,2,1,0:T(1,128)}, f32[12,7,7,1,512]{4,3,...) fusion(f32[12,7,7,9,512]{4,3,2,1,0:T(8,128)} %reshape.76), kind=kLoop, calls=%fused_computation.86 | loop fusion | bytes 21676032 | tf_op jit(solution)/shard_map/slice | solution.py:323
  185.4 1.9 copy_bitcast_fusion.6
  187.7 0.8 pad_add_fusion
  189.8 0.8 copy-done.6
  191.1 0.8 copy-done.11
  192.2 2.2 pad_add_fusion.1
  194.4 1.7 reshape.77
  196.1 1.7 fusion.2
  198.4 6.8 %exchange_5.1 = f32[2,512]{1,0:T(2,128)} custom-call(f32[2,512]{1,0:T(2,128)} %pad_maximum_fusion.8.value_ref), custom_call_target="tpu_custom_call" | custom-call | tf_op jit(solution)/shard_map/exchange_5/pallas_call | solution.py:56
  205.2 0.8 fusion.9
  206.0 0.6 pad_maximum_fusion.value_ref
  206.7 7.3 %exchange_6.1 = f32[2,3072]{1,0:T(2,128)} custom-call(f32[2,3072]{1,0:T(2,128)} %pad_maximum_fusion.value_ref), custom_call_target="tpu_custom_call" | custom-call | tf_op jit(solution)/shard_map/exchange_6/pallas_call | solution.py:56
  214.0 1.4 broadcast_multiply_fusion
  215.3 2.4 multiply_convert_fusion.2.grad_one
  217.8 20.1 %weight_products.1.grads = f32[512,8704]{1,0:T(8,128)} custom-call(bf16[588,512]{1,0:T(8,128)(2,1)} %multiply_convert_fusion.2.grad_one, bf16[588,2048]{1,0:T(8,128)(2,1)} %reshape.73.flat_in, bf16[588,512]{1,0:T(8,128)(2,1)} %copy-done.3, bf16[588,4608]{1,0:T(8,128)(2,1)} %constant_dynamic-update-slice_fusion.patches, bf16[588,512]{1,0:T(8,128)(2,1)} %copy-done.12, ...), custom_call_target="tpu_custom_call" | custom-call | tf_op jit(solution)/shard_map/weight_products/pallas_call | solution.py:96
  237.9 90.3 %scatter_sum.1 = f32[64,2176]{1,0:T(8,128)} custom-call(f32[512,8704]{1,0:T(8,128)} %weight_products.1.grads), custom_call_target="tpu_custom_call" | custom-call | tf_op jit(solution)/shard_map/scatter_sum/pallas_call | solution.py:263
  328.3 5.9 %add_convert_fusion = bf16[588,2048]{1,0:T(8,128)(2,1)} fusion(f32[588,2048]{1,0:T(8,128)} %get-tuple-element.17, bf16[588,512]{1,0:T(8,128)(2,1)S(1)} %copy-done.4, bf16[2048,512]{1,0:T(8,128)(2,1)} %param.9), kind=kOutput, calls=%fused_computation | convolution fusion | flops 1235533824 | bytes 9924608 | tf_op jit(solution)/shard_map/dot_general | solution.py:20
  334.2 4.2 %reshape.78 = bf16[12,7,7,2048]{3,2,1,0:T(8,128)(2,1)} reshape(bf16[588,2048]{1,0:T(8,128)(2,1)} %add_convert_fusion) | data formatting | bytes 4816896 | tf_op jit(solution)/shard_map/reshape | solution.py:389
  338.4 4.4 %reshape.75 = bf16[12,7,7,2048]{3,2,1,0:T(8,128)(2,1)} reshape(bf16[588,2048]{1,0:T(8,128)(2,1)} %get-tuple-element.27) | data formatting | bytes 4816896 | tf_op jit(solution)/shard_map/reshape | solution.py:388
  342.7 0.8 copy.56
  (46 shorter events, 4.8 us)
Async XLA Ops:
  0.6 78.4 %copy-start = (bf16[2048,512]{1,0:T(8,128)(2,1)S(1)}, bf16[2048,512]{1,0:T(8,128)(2,1)}, u32[]{:S(2)}) copy-start(bf16[2048,512]{1,0:T(8,128)(2,1)} %param.11) | copy-start | bytes 6291460
  5.0 13.8 %copy-start.14 = (f32[3072]{0:T(1024)S(1)}, f32[3072]{0:T(1024)}, u32[]{:S(2)}) copy-start(f32[3072]{0:T(1024)} %param.13) | copy-start | bytes 36868
  5.0 13.8 %copy-start.15 = (f32[3072]{0:T(1024)S(1)}, f32[3072]{0:T(1024)}, u32[]{:S(2)}) copy-start(f32[3072]{0:T(1024)} %param.12) | copy-start | bytes 36868
  79.1 3.7 %copy-start.12 = (bf16[588,512]{1,0:T(8,128)(2,1)}, bf16[588,512]{1,0:T(8,128)(2,1)S(1)}, u32[]{:S(2)}) copy-start(bf16[588,512]{1,0:T(8,128)(2,1)S(1)} %multiply_convert_fusion.4.hidden_two) | copy-start | bytes 1806340
  91.5 4.6 %slice-start = ((f32[3072]{0:T(1024)}), f32[2048]{0:T(1024)S(1)}, s32[]{:S(2)}) async-start(f32[3072]{0:T(1024)} %param.13), calls=%async_computation | async-start | bytes 16384 | tf_op jit(solution)/shard_map/slice | solution.py:345
  112.8 5.2 %copy-start.5 = (f32[588,512]{1,0:T(8,128)S(1)}, f32[588,512]{1,0:T(8,128)}, u32[]{:S(2)}) copy-start(f32[588,512]{1,0:T(8,128)} %get-tuple-element.59) | copy-start | bytes 3612676
  118.1 2.9 copy-start.2
  131.1 8.3 %copy-start.3 = (bf16[588,512]{1,0:T(8,128)(2,1)}, bf16[588,512]{1,0:T(8,128)(2,1)S(1)}, u32[]{:S(2)}) copy-start(bf16[588,512]{1,0:T(8,128)(2,1)S(1)} %multiply_convert_fusion.3.grad_two) | copy-start | bytes 1806340
  185.3 2.0 copy-start.9
  185.4 2.0 copy-start.10
  187.7 1.3 copy-start.7
  187.7 1.6 copy-start.8
  189.4 1.3 copy-start.6
  190.6 1.3 copy-start.11
  237.9 90.3 %copy-start.4 = (bf16[588,512]{1,0:T(8,128)(2,1)S(1)}, bf16[588,512]{1,0:T(8,128)(2,1)}, u32[]{:S(2)}) copy-start(bf16[588,512]{1,0:T(8,128)(2,1)} %multiply_convert_fusion.2.grad_one) | copy-start | bytes 1806340
  338.4 4.4 %copy-start.13 = (f32[64,2176]{1,0:T(8,128)S(1)}, f32[64,2176]{1,0:T(8,128)}, u32[]{:S(2)}) copy-start(f32[64,2176]{1,0:T(8,128)} %scatter_sum.1) | copy-start | bytes 1671172
  338.4 5.2 %copy-start.1 = (bf16[2048,512]{1,0:T(8,128)(2,1)S(1)}, bf16[2048,512]{1,0:T(8,128)(2,1)}, u32[]{:S(2)}) copy-start(bf16[2048,512]{1,0:T(8,128)(2,1)} %param.11) | copy-start | bytes 6291460

commit v2 on v1

--- a/solution.py
+++ b/solution.py
@@ -68,8 +68,9 @@
     )(value)
 
 
-def weight_kernel(starts, grad_one, flat_in, grad_two, patches, hidden_two, grad_three, out_ref):
+def weight_kernel(starts, stride, grad_one, flat_in, grad_two, shifted, hidden_two, grad_three, out_ref):
     at = pl.program_id(0)
+    rows = grad_two.shape[0]
 
     @pl.when(at < starts[0])
     def _():
@@ -77,16 +78,20 @@
 
     @pl.when(jnp.logical_and(at >= starts[0], at < starts[1]))
     def _():
-        out_ref[...] = contract(grad_two[...], patches[...], 0, 0)
+        tap = at - starts[0]
+        first = pl.multiple_of((tap // 3) * stride, 16)
+        window = shifted[lax.rem(tap, 3), pl.ds(first, rows), :]
+        out_ref[...] = contract(grad_two[...], window, 0, 0)
 
     @pl.when(at >= starts[1])
     def _():
         out_ref[...] = contract(hidden_two[...], grad_three[...], 0, 0)
 
 
-def weight_products(grad_one, flat_in, grad_two, patches, hidden_two, grad_three):
+def weight_products(grad_one, flat_in, grad_two, shifted, hidden_two, grad_three):
     rows, mid = grad_one.shape
-    counts = [array.shape[1] // mid for array in (flat_in, patches, grad_three)]
+    stride = (shifted.shape[1] - rows) // 2
+    counts = [flat_in.shape[1] // mid, 9, grad_three.shape[1] // mid]
     starts = (counts[0], counts[0] + counts[1])
     whole = pl.BlockSpec((rows, mid), lambda at: (0, 0))
 
@@ -94,20 +99,61 @@
         return pl.BlockSpec((rows, mid), lambda at: (0, jnp.clip(at - first, 0, count - 1)))
 
     return pl.pallas_call(
-        functools.partial(weight_kernel, starts),
+        functools.partial(weight_kernel, starts, stride),
         grid=(sum(counts),),
         out_shape=jax.ShapeDtypeStruct((mid, sum(counts) * mid), jnp.float32),
         in_specs=[
             whole,
             columns(0, counts[0]),
             whole,
-            columns(starts[0], counts[1]),
+            pl.BlockSpec(shifted.shape, lambda at: (0, 0, 0)),
             whole,
             columns(starts[1], counts[2]),
         ],
         out_specs=pl.BlockSpec((mid, mid), lambda at: (0, at)),
         name="weight_products",
-    )(grad_one, flat_in, grad_two, patches, hidden_two, grad_three)
+    )(grad_one, flat_in, grad_two, shifted, hidden_two, grad_three)
+
+
+def conv_kernel(mirror, width, padded, field, weights, out_ref, shifted):
+    rows, mid = field.shape
+    stride = (shifted.shape[1] - rows) // 2
+    values = field[...].astype(jnp.float32)
+    for col_tap in range(3):
+        moved = values if col_tap == 1 else pltpu.roll(values, (1 - col_tap) % rows, 0)
+        shifted[col_tap, :stride, :] = jnp.zeros((stride, mid), shifted.dtype)
+        shifted[col_tap, stride + rows :, :] = jnp.zeros((stride, mid), shifted.dtype)
+        shifted[col_tap, stride : stride + rows, :] = moved.astype(shifted.dtype)
+    out_ref[...] = jnp.zeros_like(out_ref)
+
+    def step(tap, carry):
+        row_tap, col_tap = tap // 3, lax.rem(tap, 3)
+        if mirror:
+            row_tap, col_tap = 2 - row_tap, 2 - col_tap
+        window = shifted[col_tap, pl.ds(pl.multiple_of(row_tap * stride, 16), rows), :]
+        block = weights[pl.ds(pl.multiple_of(tap * mid, 16), mid), :]
+        out_ref[...] += contract(window, block, 1, 1 if mirror else 0)
+        return carry
+
+    lax.fori_loop(0, 9, step, 0)
+    column = lax.rem(lax.broadcasted_iota(jnp.int32, (rows, mid), 0), padded)
+    out_ref[...] = jnp.where(column < width, out_ref[...], 0.0)
+
+
+def convolve(field, weights, images_count, width, padded, mirror):
+    rows, mid = field.shape
+    stride = images_count * padded
+    return pl.pallas_call(
+        functools.partial(conv_kernel, mirror, width, padded),
+        out_shape=(
+            jax.ShapeDtypeStruct((rows, mid), jnp.float32),
+            jax.ShapeDtypeStruct((3, rows + 2 * stride, mid), field.dtype),
+        ),
+        in_specs=[pl.BlockSpec(memory_space=pltpu.VMEM)] * 2,
+        out_specs=[pl.BlockSpec(memory_space=pltpu.VMEM)] * 2,
+        compiler_params=pltpu.CompilerParams(vmem_limit_bytes=40 * 1024 * 1024),
+        name="convolve_back" if mirror else "convolve",
+    )(field, weights)
 
 
 def scatter_plan(n_group, n_rep, rows):
@@ -284,8 +330,7 @@
     return sigma * (1.0 + value * (1.0 - sigma))
 
 
-def normalize(pre_norm, norm_gain, norm_shift, group_size, ident):
-    number = pre_norm.shape[0] * group_size
+def normalize(pre_norm, norm_gain, norm_shift, number, ident):
     sums = jnp.stack([jnp.sum(pre_norm, axis=0), jnp.sum(pre_norm * pre_norm, axis=0)])
     first_sum, second_sum = exchange_sum(sums, "bngroup", ident)
     centre = first_sum / number
@@ -295,35 +340,23 @@
     return (scaled, inverse, norm_gain * scaled + norm_shift)
 
 
-def norm_back(upstream, scaled, inverse, norm_gain, group_size, ident):
+def norm_back(upstream, scaled, inverse, norm_gain, real, number, ident):
     sums = jnp.stack([jnp.sum(upstream, axis=0), jnp.sum(upstream * scaled, axis=0)])
     shift_sum, gain_sum = exchange_sum(sums, "bngroup", ident)
-    number = upstream.shape[0] * group_size
     result = norm_gain * inverse * (upstream - shift_sum / number - scaled * gain_sum / number)
+    result = jnp.where(real, result, 0.0)
     return (result.astype(jnp.bfloat16), shift_sum, gain_sum)
 
 
-def unfold(field):
-    length = field.shape[1]
-    padded = jnp.pad(field, ((0, 0), (1, 1), (1, 1), (0, 0)))
-    windows = [
-        padded[:, row_tap : row_tap + length, col_tap : col_tap + length, :]
-        for row_tap in range(3)
-        for col_tap in range(3)
-    ]
-    return jnp.concatenate(windows, axis=-1).reshape(-1, 9 * field.shape[3])
-
-
-def fold_back(columns, images_count, length, channels):
-    shaped = columns.reshape(images_count, length, length, 9, channels)
-    summed = jnp.zeros((images_count, length + 2, length + 2, channels), jnp.float32)
-    for row_tap in range(3):
-        for col_tap in range(3):
-            summed = summed + jnp.pad(
-                shaped[:, :, :, 3 * row_tap + col_tap, :],
-                ((0, 0), (row_tap, 2 - row_tap), (col_tap, 2 - col_tap), (0, 0)),
-            )
-    return summed[:, 1 : length + 1, 1 : length + 1, :].reshape(-1, channels)
+def to_rows(field, padded):
+    turned = field.transpose(1, 0, 2, 3)
+    turned = jnp.pad(turned, ((0, 0), (0, 0), (0, padded - field.shape[2]), (0, 0)))
+    return turned.reshape(-1, field.shape[3])
+
+
+def from_rows(rows, shape, padded):
+    turned = rows.reshape(shape[1], shape[0], padded, shape[3])
+    return turned[:, :, : shape[2], :].transpose(1, 0, 2, 3)
 
 
 def per_device(images, cotangent, w_reduce, w_spatial, w_expand, norm_gain, norm_shift):
@@ -333,7 +366,10 @@
     length = images.shape[1]
     wide_ch = images.shape[3]
     mid_ch = w_reduce.shape[1]
-    flat_in = images.reshape(-1, wide_ch)
+    padded = (images.shape[2] // 8 + 1) * 8
+    number = images_count * length * images.shape[2] * group_size
+    flat_in = to_rows(images, padded)
+    real = (jnp.arange(flat_in.shape[0]) % padded < images.shape[2])[:, None]
     gain_one, gain_two, gain_three = (
         norm_gain[:mid_ch],
         norm_gain[mid_ch : 2 * mid_ch],
@@ -345,36 +381,37 @@
         norm_shift[2 * mid_ch :],
     )
     scaled_one, inverse_one, normed_one = normalize(
-        matmul(flat_in, w_reduce), gain_one, shift_one, group_size, 0
-    )
-    hidden_one = jax.nn.silu(normed_one).astype(jnp.bfloat16)
-    patches = unfold(hidden_one.reshape(images_count, length, length, mid_ch))
+        matmul(flat_in, w_reduce), gain_one, shift_one, number, 0
+    )
+    hidden_one = jnp.where(real, jax.nn.silu(normed_one), 0.0).astype(jnp.bfloat16)
+    spatial_pre, shifted = convolve(
+        hidden_one, w_spatial, images_count, images.shape[2], padded, False
+    )
     scaled_two, inverse_two, normed_two = normalize(
-        matmul(patches, w_spatial), gain_two, shift_two, group_size, 1
-    )
-    hidden_two = jax.nn.silu(normed_two).astype(jnp.bfloat16)
+        spatial_pre, gain_two, shift_two, number, 1
+    )
+    hidden_two = jnp.where(real, jax.nn.silu(normed_two), 0.0).astype(jnp.bfloat16)
     scaled_three, inverse_three, normed_three = normalize(
-        contract(hidden_two, w_expand, 1, 1), gain_three, shift_three, group_size, 2
+        contract(hidden_two, w_expand, 1, 1), gain_three, shift_three, number, 2
     )
     summed_in = normed_three + flat_in.astype(jnp.float32)
     output = jax.nn.silu(summed_in).astype(jnp.bfloat16)
-    upstream = cotangent.reshape(-1, wide_ch).astype(jnp.float32) * slope(summed_in)
+    upstream = to_rows(cotangent, padded).astype(jnp.float32) * slope(summed_in)
     grad_three, shift_sum_three, gain_sum_three = norm_back(
-        upstream, scaled_three, inverse_three, gain_three, group_size, 3
+        upstream, scaled_three, inverse_three, gain_three, real, number, 3
     )
     back_two = matmul(grad_three, w_expand) * slope(normed_two)
     grad_two, shift_sum_two, gain_sum_two = norm_back(
-        back_two, scaled_two, inverse_two, gain_two, group_size, 4
-    )
-    back_one = fold_back(contract(grad_two, w_spatial, 1, 1), images_count, length, mid_ch) * slope(
-        normed_one
-    )
+        back_two, scaled_two, inverse_two, gain_two, real, number, 4
+    )
+    spatial_back, _ = convolve(grad_two, w_spatial, images_count, images.shape[2], padded, True)
+    back_one = spatial_back * slope(normed_one)
     grad_one, shift_sum_one, gain_sum_one = norm_back(
-        back_one, scaled_one, inverse_one, gain_one, group_size, 5
+        back_one, scaled_one, inverse_one, gain_one, real, number, 5
     )
     in_grad = (upstream + contract(grad_one, w_reduce, 1, 1)).astype(jnp.bfloat16)
     local_grads = weight_products(
-        grad_one, flat_in, grad_two, patches, hidden_two, grad_three
+        grad_one, flat_in, grad_two, shifted, hidden_two, grad_three
     )
     summed_grads = scatter_sum(local_grads, images_total, 7).T
     group_norms = jnp.stack(
@@ -385,8 +422,8 @@
     )
     norm_summed = exchange_sum(group_norms, "rep", 6)
     return (
-        output.reshape(images.shape),
-        in_grad.reshape(images.shape),
+        from_rows(output, images.shape, padded),
+        from_rows(in_grad, images.shape, padded),
         summed_grads,
         norm_summed / images_total,
     )

time: 346 us -> 244 us (0.71)
  local copies, waits for them, and re-layouts: 112 us -> 20.6 us
  matrix products: 32.4 us -> 15 us
  Pallas kernels: 162 us -> 172 us
    slice x2 -> x0, local copies, waits for them, and re-layouts: 37.5 us -> none  [the longest x1 32 us: fold_back(): shaped[:, :, :, 3 * row_tap + col_tap, :]]
    reshape x6 -> x0, local copies, waits for them, and re-layouts: 30.6 us -> none  [the longest x1 13.9 us: fold_back(): shaped = columns.reshape(images_count, length, length, 9, channels)]
    concatenate x9 -> x0, local copies, waits for them, and re-layouts: 18.5 us -> none  [unfold(): return jnp.concatenate(windows, axis=-1).reshape(-1, 9 * field.shape[3])]
    pallas_call x1 -> x3, Pallas kernels: 20.1 us -> 30.8 us  [the longest x1 19 us: weight_products(): pl.pallas_call(functools.partial(weight_kernel, starts, stride), grid=(su...]
    dot_general x3 -> x2, matrix products: 14.6 us -> 4.74 us  [matmul(): return jnp.dot(left, right, preferred_element_type=jnp.float32)]
    dot_general x3 -> x2, matrix products: 17.8 us -> 10.2 us  [contract(): lax.dot_general(left, right, (((left_dim,), (right_dim,)), ((), ())), pre...]
    unnamed x41 -> x46, local copies, waits for them, and re-layouts: 17.3 us -> 11.1 us
    transpose x0 -> x1, local copies, waits for them, and re-layouts: none -> 4.13 us  [from_rows(): return turned[:, :, :shape[2], :].transpose(1, 0, 2, 3)]
where the time goes in v2:
time: 244 us; the launch traced here: 243 us
  Pallas kernels  172 us (70%)
  other arithmetic  34.5 us (14%)
  local copies, waits for them, and re-layouts  20.6 us (8%)
  matrix products  15 us (6%)
    pallas_call x1, Pallas kernels, scatter_sum(): pl.pallas_call(functools.partial(scatter_kernel, n_group, n_rep, 1.0 / im...  90.3 us
    pallas_call x7, Pallas kernels, exchange_sum(): pl.pallas_call(functools.partial(exchange_kernel, axis, size), out_shape=...  51 us
    pallas_call x1, Pallas kernels, weight_products(): pl.pallas_call(functools.partial(weight_kernel, starts, stride), grid=(su...  19 us
    pallas_call x2, Pallas kernels, convolve(): pl.pallas_call(functools.partial(conv_kernel, mirror, width, padded), out...  11.9 us
    unnamed x46, local copies, waits for them, and re-layouts  11.1 us
    reduce_sum x2, other arithmetic, norm_back(): jnp.sum(upstream, axis=0)  10.6 us
    dot_general x2, matrix products, contract(): lax.dot_general(left, right, (((left_dim,), (right_dim,)), ((), ())), pre...  10.2 us
    convert_element_type x3, other arithmetic, norm_back(): return (result.astype(jnp.bfloat16), shift_sum, gain_sum)  8.85 us

profile of v2, /device:TPU:0, one launch (start us, length us, event | category | flops | bytes accessed | tf_op | source)
XLA Modules:
  0.0 243.1 jit_solution(9304184932340229728)
XLA Ops:
  0.6 0.0 copy-start
  0.7 0.8 slice.26
  1.5 0.8 fusion.11
  2.3 2.0 copy.17
  4.2 0.0 copy-start.13
  4.2 0.7 pad.7.clone
  5.0 0.0 copy-start.6
  5.0 0.8 copy-done.13
  5.8 1.6 fusion.9
  7.4 0.0 copy-done.6
  7.4 0.0 copy-start.7
  7.5 0.7 pad_maximum_fusion.5.value_ref
  8.1 8.6 %exchange_0.1 = f32[2,512]{1,0:T(2,128)} custom-call(f32[2,512]{1,0:T(2,128)} %pad_maximum_fusion.5.value_ref), custom_call_target="tpu_custom_call" | custom-call | tf_op jit(solution)/shard_map/exchange_0/pallas_call | solution.py:56
  16.7 0.8 slice_multiply_fusion.2
  17.5 0.0 copy-done.7
  17.5 0.5 select_convert_fusion.4.field
  18.0 0.0 copy-start.2
  18.0 2.3 copy-done.2
  20.4 5.4 %convolve.1 = (f32[672,512]{1,0:T(8,128)S(1)}, bf16[3,864,512]{2,1,0:T(8,128)(2,1)S(1)}) custom-call(bf16[672,512]{1,0:T(8,128)(2,1)S(1)} %select_convert_fusion.4.field, bf16[4608,512]{1,0:T(8,128)(2,1)S(1)} %copy-done.2), custom_call_target="tpu_custom_call" | custom-call | tf_op jit(solution)/shard_map/convolve/pallas_call | solution.py:146
  25.8 0.0 copy-start.5
  25.8 1.5 copy-done.5
  27.4 0.2 fusion.8
  27.6 0.6 pad_maximum_fusion.6.value_ref
  28.2 6.8 %exchange_1.1 = f32[2,512]{1,0:T(2,128)} custom-call(f32[2,512]{1,0:T(2,128)} %pad_maximum_fusion.6.value_ref), custom_call_target="tpu_custom_call" | custom-call | tf_op jit(solution)/shard_map/exchange_1/pallas_call | solution.py:56
  35.0 0.8 slice_multiply_fusion.1
  35.8 0.0 copy-done.15
  35.8 0.6 slice_multiply_fusion.3
  36.4 0.5 select_convert_fusion.3.hidden_two
  36.9 2.8 %pad_convert_fusion = f32[7,12,8,2048]{3,2,0,1:T(8,128)S(1)} fusion(bf16[7,12,7,2048]{3,2,0,1:T(8,128)(2,1)} %bitcast.58), kind=kLoop, calls=%fused_computation.11 | loop fusion | flops 1376256 | bytes 7913472 | tf_op jit(solution)/shard_map/convert_element_type | solution.py:399
  39.7 3.0 %copy.13 = f32[7,12,8,2048]{3,2,1,0:T(8,128)} copy(f32[7,12,8,2048]{3,2,0,1:T(8,128)S(1)} %pad_convert_fusion) | data formatting | bytes 11010048 | tf_op jit(solution)/shard_map/convert_element_type | solution.py:399
  42.7 4.1 %fusion.5 = (f32[2048]{0:T(1024)S(1)}, f32[2048]{0:T(1024)S(1)}, f32[672,2048]{1,0:T(8,128)}) fusion(bf16[672,512]{1,0:T(8,128)(2,1)S(1)} %select_convert_fusion.3.hidden_two, bf16[2048,512]{1,0:T(8,128)(2,1)S(1)} %copy-done), kind=kOutput, calls=%fused_computation.57 | convolution fusion | flops 1413410816 | bytes 8306688 | tf_op jit(solution)/shard_map/dot_general | solution.py:20
  46.8 0.6 pad_maximum_fusion.1.value_ref
  47.5 7.3 %exchange_2.1 = f32[2,2048]{1,0:T(2,128)} custom-call(f32[2,2048]{1,0:T(2,128)} %pad_maximum_fusion.1.value_ref), custom_call_target="tpu_custom_call" | custom-call | tf_op jit(solution)/shard_map/exchange_2/pallas_call | solution.py:56
  54.8 0.8 slice_multiply_fusion
  55.6 0.0 slice-done
  55.6 8.8 %fusion.4 = (f32[2048]{0:T(1024)S(1)}, f32[2048]{0:T(1024)S(1)}, f32[672,2048]{1,0:T(8,128)}, bf16[672,2048]{1,0:T(8,128)(2,1)}) fusion(f32[2048]{0:T(1024)S(1)} %bitcast.61, f32[672,2048]{1,0:T(8,128)} %get-tuple-element.48, f32[2048]{0:T(1024)S(1)} %bitcast.63, bf16[7,12,8,2048]{3,2,1,0:T(8,128)(2,1)} %copy-done.6, f32[2048]{0:T(1024)S(1)} %slice-done, ...), kind=kLoop, calls=%fused_computation.56 | loop fusion | flops 26144768 | bytes 22069248 | tf_op jit(solution)/shard_map/reduce_sum | solution.py:344
  64.4 0.6 pad_maximum_fusion.2.value_ref
  65.1 7.3 %exchange_3.1 = f32[2,2048]{1,0:T(2,128)} custom-call(f32[2,2048]{1,0:T(2,128)} %pad_maximum_fusion.2.value_ref), custom_call_target="tpu_custom_call" | custom-call | tf_op jit(solution)/shard_map/exchange_3/pallas_call | solution.py:56
  72.4 0.8 fusion.10
  73.2 0.0 copy-start.19
  73.2 5.2 %select_convert_fusion.grad_three = bf16[672,2048]{1,0:T(8,128)(2,1)S(1)} fusion(f32[672,2048]{1,0:T(8,128)} %get-tuple-element.23, f32[672,2048]{1,0:T(8,128)} %get-tuple-element.48, f32[2048]{0:T(1024)S(1)} %bitcast.65, f32[2048]{0:T(1024)S(1)} %bitcast.73, f32[2048]{0:T(1024)S(1)} %get-tuple-element.33, f32[2048]{0:T(1024)S(1)} %bitcast.62, ...), kind=kLoop, calls=%fused_computation.2 | loop fusion | flops 12386304 | bytes 13804192 | tf_op jit(solution)/shard_map/convert_element_type | solution.py:348
  78.4 3.1 %fusion.7 = (f32[512]{0:T(512)S(1)}, f32[512]{0:T(512)S(1)}, f32[672,512]{1,0:T(8,128)}) fusion(f32[512]{0:T(512)S(1)} %bitcast.82, f32[672,512]{1,0:T(8,128)S(1)} %get-tuple-element.7, f32[512]{0:T(512)S(1)} %bitcast.85, f32[512]{0:T(512)S(1)} %copy-done.19, f32[512]{0:T(512)S(1)} %copy-done.17, bf16[672,2048]{1,0:T(8,128)(2,1)S(1)} %select_convert_fusion.grad_three, ...), kind=kOutput, calls=%fused_computation.59 | convolution fusion | flops 1414446080 | bytes 7614464 | tf_op jit(solution)/shard_map/dot_general | solution.py:16
  81.6 0.6 pad_maximum_fusion.7.value_ref
  82.2 6.8 %exchange_4.1 = f32[2,512]{1,0:T(2,128)} custom-call(f32[2,512]{1,0:T(2,128)} %pad_maximum_fusion.7.value_ref), custom_call_target="tpu_custom_call" | custom-call | tf_op jit(solution)/shard_map/exchange_4/pallas_call | solution.py:56
  89.0 0.8 fusion.13
  89.8 1.8 select_convert_fusion.2.field.grad_two
  91.5 0.0 copy-start.3
  91.6 2.3 copy-done.3
  93.9 6.4 %convolve_back.1 = (f32[672,512]{1,0:T(8,128)S(1)}, bf16[3,864,512]{2,1,0:T(8,128)(2,1)}) custom-call(bf16[672,512]{1,0:T(8,128)(2,1)S(1)} %select_convert_fusion.2.field.grad_two, bf16[4608,512]{1,0:T(8,128)(2,1)S(1)} %copy-done.3), custom_call_target="tpu_custom_call" | custom-call | tf_op jit(solution)/shard_map/convolve_back/pallas_call | solution.py:146
  100.3 1.8 fusion.6
  102.1 0.6 pad_maximum_fusion.8.value_ref
  102.7 6.8 %exchange_5.1 = f32[2,512]{1,0:T(2,128)} custom-call(f32[2,512]{1,0:T(2,128)} %pad_maximum_fusion.8.value_ref), custom_call_target="tpu_custom_call" | custom-call | tf_op jit(solution)/shard_map/exchange_5/pallas_call | solution.py:56
  109.6 0.8 fusion.12
  110.4 0.0 copy-start.14
  110.4 1.9 select_convert_fusion.1.grad_one
  112.3 0.1 copy-done.14
  112.4 6.1 %add_convert_fusion = bf16[672,2048]{1,0:T(8,128)(2,1)} fusion(f32[672,2048]{1,0:T(8,128)} %get-tuple-element.23, bf16[672,512]{1,0:T(8,128)(2,1)S(1)} %select_convert_fusion.1.grad_one, bf16[2048,512]{1,0:T(8,128)(2,1)S(1)} %copy-done.14), kind=kOutput, calls=%fused_computation.1 | convolution fusion | flops 1412038656 | bytes 11042816 | tf_op jit(solution)/shard_map/dot_general | solution.py:20
  118.5 0.6 pad_maximum_fusion.value_ref
  119.1 7.3 %exchange_6.1 = f32[2,3072]{1,0:T(2,128)} custom-call(f32[2,3072]{1,0:T(2,128)} %pad_maximum_fusion.value_ref), custom_call_target="tpu_custom_call" | custom-call | tf_op jit(solution)/shard_map/exchange_6/pallas_call | solution.py:56
  126.5 1.4 broadcast_multiply_fusion
  127.8 4.1 %copy_bitcast_fusion = (bf16[12,7,7,2048]{3,2,1,0:T(8,128)(2,1)}, bf16[12,7,7,2048]{3,2,1,0:T(8,128)(2,1)}) fusion(bf16[7,12,8,2048]{3,2,1,0:T(8,128)(2,1)S(1)} %bitcast.55, bf16[7,12,8,2048]{3,2,1,0:T(8,128)(2,1)} %bitcast.56), kind=kLoop, calls=%fused_computation.9 | loop fusion | bytes 10321920 | tf_op jit(solution)/shard_map/transpose | solution.py:359
  132.0 19.0 %weight_products.1.grads = f32[512,8704]{1,0:T(8,128)} custom-call(bf16[672,512]{1,0:T(8,128)(2,1)} %copy-done.11, bf16[672,2048]{1,0:T(8,128)(2,1)} %bitcast.54, bf16[672,512]{1,0:T(8,128)(2,1)} %copy-done.4, bf16[3,864,512]{2,1,0:T(8,128)(2,1)} %copy-done.5, bf16[672,512]{1,0:T(8,128)(2,1)} %copy-done.12, bf16[672,2048]{1,0:T(8,128)(2,1)} %copy-done.10), custom_call_target="tpu_custom_call" | custom-call | tf_op jit(solution)/shard_map/weight_products/pallas_call | solution.py:101
  150.9 90.3 %scatter_sum.1 = f32[64,2176]{1,0:T(8,128)} custom-call(f32[512,8704]{1,0:T(8,128)} %weight_products.1.grads), custom_call_target="tpu_custom_call" | custom-call | tf_op jit(solution)/shard_map/scatter_sum/pallas_call | solution.py:309
  241.2 1.9 copy.21
  (32 shorter events, 0.1 us)
Async XLA Ops:
  0.6 42.1 %copy-start = (bf16[2048,512]{1,0:T(8,128)(2,1)S(1)}, bf16[2048,512]{1,0:T(8,128)(2,1)}, u32[]{:S(2)}) copy-start(bf16[2048,512]{1,0:T(8,128)(2,1)} %param.11) | copy-start | bytes 6291460
  2.3 34.1 %copy-start.18 = (f32[512]{0:T(512)}, f32[512]{0:T(512)S(1)}, u32[]{:S(2)}) copy-start(f32[512]{0:T(512)S(1)} %get-tuple-element.35) | copy-start | bytes 6148
  4.2 1.6 copy-start.13
  5.0 2.4 %copy-start.6 = (bf16[7,12,8,2048]{3,2,1,0:T(8,128)(2,1)}, bf16[7,12,8,2048]{3,2,1,0:T(8,128)(2,1)S(1)}, u32[]{:S(2)}) copy-start(bf16[7,12,8,2048]{3,2,1,0:T(8,128)(2,1)S(1)} %pad.7.clone) | copy-start | bytes 8257540
  7.4 10.1 %copy-start.7 = (f32[672,512]{1,0:T(8,128)}, f32[672,512]{1,0:T(8,128)S(1)}, u32[]{:S(2)}) copy-start(f32[672,512]{1,0:T(8,128)S(1)} %get-tuple-element.47) | copy-start | bytes 4128772
  18.0 2.3 copy-start.2
  25.8 1.5 copy-start.5
  27.4 8.4 %copy-start.15 = (f32[3072]{0:T(1024)S(1)}, f32[3072]{0:T(1024)}, u32[]{:S(2)}) copy-start(f32[3072]{0:T(1024)} %param.12) | copy-start | bytes 36868
  36.4 3.3 %copy-start.16 = (f32[512]{0:T(512)}, f32[512]{0:T(512)S(1)}, u32[]{:S(2)}) copy-start(f32[512]{0:T(512)S(1)} %get-tuple-element.32) | copy-start | bytes 6148
  36.9 5.8 %copy-start.12 = (bf16[672,512]{1,0:T(8,128)(2,1)}, bf16[672,512]{1,0:T(8,128)(2,1)S(1)}, u32[]{:S(2)}) copy-start(bf16[672,512]{1,0:T(8,128)(2,1)S(1)} %select_convert_fusion.3.hidden_two) | copy-start | bytes 2064388
  42.7 12.9 %slice-start = ((f32[3072]{0:T(1024)}), f32[2048]{0:T(1024)S(1)}, s32[]{:S(2)}) async-start(f32[3072]{0:T(1024)} %param.13), calls=%async_computation | async-start | bytes 16384 | tf_op jit(solution)/shard_map/slice | solution.py:381
  73.2 5.2 %copy-start.17 = (f32[512]{0:T(512)S(1)}, f32[512]{0:T(512)}, u32[]{:S(2)}) copy-start(f32[512]{0:T(512)} %copy-done.16) | copy-start | bytes 6148
  73.2 5.2 %copy-start.19 = (f32[512]{0:T(512)S(1)}, f32[512]{0:T(512)}, u32[]{:S(2)}) copy-start(f32[512]{0:T(512)} %copy-done.18) | copy-start | bytes 6148
  78.4 3.2 %copy-start.10 = (bf16[672,2048]{1,0:T(8,128)(2,1)}, bf16[672,2048]{1,0:T(8,128)(2,1)S(1)}, u32[]{:S(2)}) copy-start(bf16[672,2048]{1,0:T(8,128)(2,1)S(1)} %select_convert_fusion.grad_three) | copy-start | bytes 8257540
  78.4 11.4 %copy-start.21 = (f32[512]{0:T(512)S(1)}, f32[512]{0:T(512)}, u32[]{:S(2)}) copy-start(f32[512]{0:T(512)} %get-tuple-element.31) | copy-start | bytes 6148
  91.5 2.3 copy-start.3
  93.9 6.4 %copy-start.4 = (bf16[672,512]{1,0:T(8,128)(2,1)}, bf16[672,512]{1,0:T(8,128)(2,1)S(1)}, u32[]{:S(2)}) copy-start(bf16[672,512]{1,0:T(8,128)(2,1)S(1)} %select_convert_fusion.2.field.grad_two) | copy-start | bytes 2064388
  93.9 6.4 %copy-start.8 = (f32[672,512]{1,0:T(8,128)S(1)}, f32[672,512]{1,0:T(8,128)}, u32[]{:S(2)}) copy-start(f32[672,512]{1,0:T(8,128)} %copy-done.7) | copy-start | bytes 4128772
  100.3 10.0 %copy-start.20 = (f32[512]{0:T(512)S(1)}, f32[512]{0:T(512)}, u32[]{:S(2)}) copy-start(f32[512]{0:T(512)} %get-tuple-element.30) | copy-start | bytes 6148
  110.4 2.0 copy-start.14
  112.4 6.1 %copy-start.11 = (bf16[672,512]{1,0:T(8,128)(2,1)}, bf16[672,512]{1,0:T(8,128)(2,1)S(1)}, u32[]{:S(2)}) copy-start(bf16[672,512]{1,0:T(8,128)(2,1)S(1)} %select_convert_fusion.1.grad_one) | copy-start | bytes 2064388
  112.4 15.4 %copy-start.9 = (bf16[672,2048]{1,0:T(8,128)(2,1)S(1)}, bf16[672,2048]{1,0:T(8,128)(2,1)}, u32[]{:S(2)}) copy-start(bf16[672,2048]{1,0:T(8,128)(2,1)} %get-tuple-element.24) | copy-start | bytes 8257540
  150.9 92.2 %copy-start.1 = (bf16[2048,512]{1,0:T(8,128)(2,1)S(1)}, bf16[2048,512]{1,0:T(8,128)(2,1)}, u32[]{:S(2)}) copy-start(bf16[2048,512]{1,0:T(8,128)(2,1)} %param.11) | copy-start | bytes 6291460

commit v3 on v2

--- a/solution.py
+++ b/solution.py
@@ -177,7 +177,9 @@
     return bits, streams
 
 
-def scatter_kernel(n_group, n_rep, scale, grads, out_ref, own, got, load_sem, send_sem, recv_sem):
+def scatter_kernel(
+    n_group, n_rep, scale, grads, norms, out_ref, norm_out, own, got, load_sem, send_sem, recv_sem, slots, far_send, far_recv
+):
     rows, cols = out_ref.shape
     bits, streams = scatter_plan(n_group, n_rep, rows)
     rest = bits[1:]
@@ -193,6 +195,9 @@
     barrier = pltpu.get_barrier_semaphore()
     for axis, at in bits:
         pl.semaphore_signal(barrier, inc=1, device_id=partner(axis, at), device_id_type=MESH)
+    peers = [lax.rem(place["rep"] + step, n_rep) for step in range(1, n_rep)]
+    for peer in peers:
+        pl.semaphore_signal(barrier, inc=1, device_id={"rep": peer}, device_id_type=MESH)
 
     def source(relative, other, begin, size):
         spot = dict(place)
@@ -207,7 +212,7 @@
         return grads.at[pl.ds(first, size), pl.ds(pl.multiple_of(spot["bngroup"] * cols, 128), cols)]
 
     count = 1 << len(rest)
-    slot_of, slots = {}, count
+    slot_of = {}
     for number, (begin, size, order) in enumerate(streams):
         used = count
         active = list(range(count))
@@ -233,7 +238,20 @@
     for relative in range(count):
         for number, (begin, size, order) in enumerate(streams):
             loads[number, first_order(order)[relative]].start()
-    pl.semaphore_wait(barrier, len(bits))
+    pl.semaphore_wait(barrier, len(bits) + n_rep - 1)
+    far = []
+    for step, peer in enumerate(peers):
+        copy = pltpu.make_async_remote_copy(
+            src_ref=norms,
+            dst_ref=slots.at[place["rep"]],
+            send_sem=far_send.at[step],
+            recv_sem=far_recv.at[step],
+            device_id={"rep": peer},
+            device_id_type=MESH,
+        )
+        copy.start()
+        far.append(copy)
+    slots[place["rep"]] = norms[...]
     sent = []
     arrivals = {}
     for relative in range(count):
@@ -296,9 +314,15 @@
             onward(*pending.pop(0))
     for copy in sent:
         copy.wait_send()
-
-
-def scatter_sum(grads, images_total, ident):
+    for copy in far:
+        copy.wait()
+    total = slots[0]
+    for member in range(1, n_rep):
+        total = total + slots[member]
+    norm_out[...] = total * scale
+
+
+def scatter_sum(grads, norms, images_total, ident):
     n_group, n_rep = lax.axis_size("bngroup"), lax.axis_size("rep")
     rows, cols = grads.shape[0] // n_rep, grads.shape[1] // n_group
     if cols % 128:
@@ -308,21 +332,27 @@
     held = 2 * count - 1
     return pl.pallas_call(
         functools.partial(scatter_kernel, n_group, n_rep, 1.0 / images_total),
-        out_shape=jax.ShapeDtypeStruct((rows, cols), jnp.float32),
-        in_specs=[pl.BlockSpec(memory_space=pl.ANY)],
-        out_specs=pl.BlockSpec(memory_space=pltpu.VMEM),
+        out_shape=(
+            jax.ShapeDtypeStruct((rows, cols), jnp.float32),
+            jax.ShapeDtypeStruct(norms.shape, jnp.float32),
+        ),
+        in_specs=[pl.BlockSpec(memory_space=pl.ANY), pl.BlockSpec(memory_space=pltpu.VMEM)],
+        out_specs=[pl.BlockSpec(memory_space=pltpu.VMEM)] * 2,
         scratch_shapes=[
             pltpu.VMEM((count, rows, cols), jnp.float32),
             pltpu.VMEM((held, rows, cols), jnp.float32),
             pltpu.SemaphoreType.DMA((len(streams), count)),
             pltpu.SemaphoreType.DMA((len(streams), held)),
             pltpu.SemaphoreType.DMA((len(streams), held)),
+            pltpu.VMEM((n_rep,) + norms.shape, jnp.float32),
+            pltpu.SemaphoreType.DMA((n_rep,)),
+            pltpu.SemaphoreType.DMA((n_rep,)),
         ],
         compiler_params=pltpu.CompilerParams(
             collective_id=ident, has_side_effects=True, vmem_limit_bytes=60 * 1024 * 1024
         ),
         name="scatter_sum",
-    )(grads)
+    )(grads, norms)
 
 
 def slope(value):
@@ -413,19 +443,18 @@
     local_grads = weight_products(
         grad_one, flat_in, grad_two, shifted, hidden_two, grad_three
     )
-    summed_grads = scatter_sum(local_grads, images_total, 7).T
     group_norms = jnp.stack(
         [
             jnp.concatenate([gain_sum_one, gain_sum_two, gain_sum_three]),
             jnp.concatenate([shift_sum_one, shift_sum_two, shift_sum_three]),
         ]
     )
-    norm_summed = exchange_sum(group_norms, "rep", 6)
+    summed_grads, norm_summed = scatter_sum(local_grads, group_norms, images_total, 7)
     return (
         from_rows(output, images.shape, padded),
         from_rows(in_grad, images.shape, padded),
-        summed_grads,
-        norm_summed / images_total,
+        summed_grads.T,
+        norm_summed,
     )
 
 

time: 244 us -> 235 us (0.963)
  Pallas kernels: 172 us -> 166 us
    pallas_call x7 -> x6, Pallas kernels: 51 us -> 43.7 us  [exchange_sum(): pl.pallas_call(functools.partial(exchange_kernel, axis, size), out_shape=...]
    unnamed x46 -> x47, local copies, waits for them, and re-layouts: 11.1 us -> 12.4 us
where the time goes in v3:
time: 235 us; the launch traced here: 234 us
  Pallas kernels  166 us (71%)
  other arithmetic  33 us (14%)
  local copies, waits for them, and re-layouts  20.5 us (9%)
  matrix products  13.4 us (6%)
    pallas_call x1, Pallas kernels, scatter_sum(): pl.pallas_call(functools.partial(scatter_kernel, n_group, n_rep, 1.0 / im...  91.2 us
    pallas_call x6, Pallas kernels, exchange_sum(): pl.pallas_call(functools.partial(exchange_kernel, axis, size), out_shape=...  43.7 us
    pallas_call x1, Pallas kernels, weight_products(): pl.pallas_call(functools.partial(weight_kernel, starts, stride), grid=(su...  18.9 us
    unnamed x47, local copies, waits for them, and re-layouts  12.4 us
    pallas_call x2, Pallas kernels, convolve(): pl.pallas_call(functools.partial(conv_kernel, mirror, width, padded), out...  11.9 us
    reduce_sum x2, other arithmetic, norm_back(): jnp.sum(upstream, axis=0)  10.6 us
    convert_element_type x3, other arithmetic, norm_back(): return (result.astype(jnp.bfloat16), shift_sum, gain_sum)  8.84 us
    dot_general x2, matrix products, contract(): lax.dot_general(left, right, (((left_dim,), (right_dim,)), ((), ())), pre...  8.66 us

profile of v3, /device:TPU:0, one launch (start us, length us, event | category | flops | bytes accessed | tf_op | source)
XLA Modules:
  0.0 233.7 jit_solution(5989018667128546374)
XLA Ops:
  0.6 0.0 copy-start
  0.7 0.8 slice.26
  1.5 0.8 fusion.11
  2.3 2.0 copy.17
  4.2 0.0 copy-start.13
  4.2 0.7 pad.7.clone
  5.0 0.0 copy-start.6
  5.0 0.8 copy-done.13
  5.8 1.6 fusion.9
  7.4 0.0 copy-done.6
  7.4 0.0 copy-start.7
  7.5 0.7 pad_maximum_fusion.5.value_ref
  8.1 8.6 %exchange_0.1 = f32[2,512]{1,0:T(2,128)} custom-call(f32[2,512]{1,0:T(2,128)} %pad_maximum_fusion.5.value_ref), custom_call_target="tpu_custom_call" | custom-call | tf_op jit(solution)/shard_map/exchange_0/pallas_call | solution.py:56
  16.7 0.8 slice_multiply_fusion.2
  17.5 0.0 copy-done.7
  17.5 0.5 select_convert_fusion.4.field
  18.0 0.0 copy-start.2
  18.0 2.3 copy-done.2
  20.3 5.4 %convolve.1 = (f32[672,512]{1,0:T(8,128)S(1)}, bf16[3,864,512]{2,1,0:T(8,128)(2,1)S(1)}) custom-call(bf16[672,512]{1,0:T(8,128)(2,1)S(1)} %select_convert_fusion.4.field, bf16[4608,512]{1,0:T(8,128)(2,1)S(1)} %copy-done.2), custom_call_target="tpu_custom_call" | custom-call | tf_op jit(solution)/shard_map/convolve/pallas_call | solution.py:146
  25.8 0.0 copy-start.5
  25.8 1.5 copy-done.5
  27.3 0.2 fusion.8
  27.5 0.6 pad_maximum_fusion.6.value_ref
  28.1 6.8 %exchange_1.1 = f32[2,512]{1,0:T(2,128)} custom-call(f32[2,512]{1,0:T(2,128)} %pad_maximum_fusion.6.value_ref), custom_call_target="tpu_custom_call" | custom-call | tf_op jit(solution)/shard_map/exchange_1/pallas_call | solution.py:56
  35.0 0.8 slice_multiply_fusion.1
  35.8 0.0 copy-done.15
  35.8 0.6 slice_multiply_fusion.3
  36.4 0.5 select_convert_fusion.3.hidden_two
  36.9 2.8 %pad_convert_fusion = f32[7,12,8,2048]{3,2,0,1:T(8,128)S(1)} fusion(bf16[7,12,7,2048]{3,2,0,1:T(8,128)(2,1)} %bitcast.58), kind=kLoop, calls=%fused_computation.11 | loop fusion | flops 1376256 | bytes 7913472 | tf_op jit(solution)/shard_map/convert_element_type | solution.py:429
  39.7 3.0 %copy.13 = f32[7,12,8,2048]{3,2,1,0:T(8,128)} copy(f32[7,12,8,2048]{3,2,0,1:T(8,128)S(1)} %pad_convert_fusion) | data formatting | bytes 11010048 | tf_op jit(solution)/shard_map/convert_element_type | solution.py:429
  42.7 0.0 copy-done
  42.7 4.1 %fusion.5 = (f32[2048]{0:T(1024)S(1)}, f32[2048]{0:T(1024)S(1)}, f32[672,2048]{1,0:T(8,128)}) fusion(bf16[672,512]{1,0:T(8,128)(2,1)S(1)} %select_convert_fusion.3.hidden_two, bf16[2048,512]{1,0:T(8,128)(2,1)S(1)} %copy-done), kind=kOutput, calls=%fused_computation.56 | convolution fusion | flops 1413410816 | bytes 8306688 | tf_op jit(solution)/shard_map/dot_general | solution.py:20
  46.8 0.6 pad_maximum_fusion.1.value_ref
  47.4 7.3 %exchange_2.1 = f32[2,2048]{1,0:T(2,128)} custom-call(f32[2,2048]{1,0:T(2,128)} %pad_maximum_fusion.1.value_ref), custom_call_target="tpu_custom_call" | custom-call | tf_op jit(solution)/shard_map/exchange_2/pallas_call | solution.py:56
  54.7 0.8 slice_multiply_fusion
  55.6 8.8 %fusion.4 = (f32[2048]{0:T(1024)S(1)}, f32[2048]{0:T(1024)S(1)}, f32[672,2048]{1,0:T(8,128)}, bf16[672,2048]{1,0:T(8,128)(2,1)}) fusion(f32[2048]{0:T(1024)S(1)} %bitcast.61, f32[672,2048]{1,0:T(8,128)} %get-tuple-element.52, f32[2048]{0:T(1024)S(1)} %bitcast.63, bf16[7,12,8,2048]{3,2,1,0:T(8,128)(2,1)} %copy-done.6, f32[2048]{0:T(1024)S(1)} %slice-done, ...), kind=kLoop, calls=%fused_computation.55 | loop fusion | flops 26144768 | bytes 22069248 | tf_op jit(solution)/shard_map/reduce_sum | solution.py:374
  64.4 0.6 pad_maximum_fusion.2.value_ref
  65.0 7.3 %exchange_3.1 = f32[2,2048]{1,0:T(2,128)} custom-call(f32[2,2048]{1,0:T(2,128)} %pad_maximum_fusion.2.value_ref), custom_call_target="tpu_custom_call" | custom-call | tf_op jit(solution)/shard_map/exchange_3/pallas_call | solution.py:56
  72.3 0.8 fusion.10
  73.1 0.0 copy-start.19
  73.1 5.2 %select_convert_fusion.grad_three = bf16[672,2048]{1,0:T(8,128)(2,1)S(1)} fusion(f32[672,2048]{1,0:T(8,128)} %get-tuple-element.27, f32[672,2048]{1,0:T(8,128)} %get-tuple-element.52, f32[2048]{0:T(1024)S(1)} %bitcast.65, f32[2048]{0:T(1024)S(1)} %bitcast.73, f32[2048]{0:T(1024)S(1)} %get-tuple-element.37, f32[2048]{0:T(1024)S(1)} %bitcast.62, ...), kind=kLoop, calls=%fused_computation.2 | loop fusion | flops 12386304 | bytes 13804192 | tf_op jit(solution)/shard_map/convert_element_type | solution.py:378
  78.3 3.1 %fusion.7 = (f32[512]{0:T(512)S(1)}, f32[512]{0:T(512)S(1)}, f32[672,512]{1,0:T(8,128)}) fusion(f32[512]{0:T(512)S(1)} %bitcast.82, f32[672,512]{1,0:T(8,128)S(1)} %get-tuple-element.9, f32[512]{0:T(512)S(1)} %bitcast.85, f32[512]{0:T(512)S(1)} %copy-done.19, f32[512]{0:T(512)S(1)} %copy-done.17, bf16[672,2048]{1,0:T(8,128)(2,1)S(1)} %select_convert_fusion.grad_three, ...), kind=kOutput, calls=%fused_computation.58 | convolution fusion | flops 1414446080 | bytes 7614464 | tf_op jit(solution)/shard_map/dot_general | solution.py:16
  81.5 0.6 pad_maximum_fusion.7.value_ref
  82.1 6.8 %exchange_4.1 = f32[2,512]{1,0:T(2,128)} custom-call(f32[2,512]{1,0:T(2,128)} %pad_maximum_fusion.7.value_ref), custom_call_target="tpu_custom_call" | custom-call | tf_op jit(solution)/shard_map/exchange_4/pallas_call | solution.py:56
  88.9 0.8 fusion.13
  89.7 1.8 select_convert_fusion.2.field.grad_two
  91.5 0.0 copy-start.3
  91.5 2.3 copy-done.3
  93.8 6.4 %convolve_back.1 = (f32[672,512]{1,0:T(8,128)S(1)}, bf16[3,864,512]{2,1,0:T(8,128)(2,1)}) custom-call(bf16[672,512]{1,0:T(8,128)(2,1)S(1)} %select_convert_fusion.2.field.grad_two, bf16[4608,512]{1,0:T(8,128)(2,1)S(1)} %copy-done.3), custom_call_target="tpu_custom_call" | custom-call | tf_op jit(solution)/shard_map/convolve_back/pallas_call | solution.py:146
  100.2 1.8 fusion.6
  102.0 0.6 pad_maximum_fusion.8.value_ref
  102.6 6.8 %exchange_5.1 = f32[2,512]{1,0:T(2,128)} custom-call(f32[2,512]{1,0:T(2,128)} %pad_maximum_fusion.8.value_ref), custom_call_target="tpu_custom_call" | custom-call | tf_op jit(solution)/shard_map/exchange_5/pallas_call | solution.py:56
  109.5 0.8 fusion.12
  110.3 0.0 copy-start.14
  110.3 1.9 select_convert_fusion.1.grad_one
  112.2 0.1 copy-done.14
  112.3 4.5 %add_convert_fusion = bf16[672,2048]{1,0:T(8,128)(2,1)S(1)} fusion(f32[672,2048]{1,0:T(8,128)} %get-tuple-element.27, bf16[672,512]{1,0:T(8,128)(2,1)S(1)} %select_convert_fusion.1.grad_one, bf16[2048,512]{1,0:T(8,128)(2,1)S(1)} %copy-done.14), kind=kOutput, calls=%fused_computation.1 | convolution fusion | flops 1412038656 | bytes 11042816 | tf_op jit(solution)/shard_map/dot_general | solution.py:20
  116.8 0.0 copy-done.11
  116.9 0.6 pad_maximum_fusion.norms
  117.5 2.8 %copy_bitcast_fusion = (bf16[12,7,7,2048]{3,2,1,0:T(8,128)(2,1)}, bf16[12,7,7,2048]{3,2,1,0:T(8,128)(2,1)}) fusion(bf16[7,12,8,2048]{3,2,1,0:T(8,128)(2,1)S(1)} %bitcast.55, bf16[7,12,8,2048]{3,2,1,0:T(8,128)(2,1)S(1)} %bitcast.56), kind=kLoop, calls=%fused_computation.9 | loop fusion | bytes 10321920 | tf_op jit(solution)/shard_map/transpose | solution.py:389
  120.3 18.9 %weight_products.1.grads = f32[512,8704]{1,0:T(8,128)} custom-call(bf16[672,512]{1,0:T(8,128)(2,1)} %copy-done.11, bf16[672,2048]{1,0:T(8,128)(2,1)} %bitcast.54, bf16[672,512]{1,0:T(8,128)(2,1)} %copy-done.4, bf16[3,864,512]{2,1,0:T(8,128)(2,1)} %copy-done.5, bf16[672,512]{1,0:T(8,128)(2,1)} %copy-done.12, bf16[672,2048]{1,0:T(8,128)(2,1)} %copy-done.10), custom_call_target="tpu_custom_call" | custom-call | tf_op jit(solution)/shard_map/weight_products/pallas_call | solution.py:101
  139.2 91.2 %scatter_sum.1 = (f32[64,2176]{1,0:T(8,128)}, f32[2,3072]{1,0:T(2,128)}) custom-call(f32[512,8704]{1,0:T(8,128)} %weight_products.1.grads, f32[2,3072]{1,0:T(2,128)} %pad_maximum_fusion.norms), custom_call_target="tpu_custom_call" | custom-call | tf_op jit(solution)/shard_map/scatter_sum/pallas_call | solution.py:333
  230.5 1.9 copy.22
  232.4 1.3 copy.23
  (31 shorter events, 0.1 us)
Async XLA Ops:
  0.6 42.0 %copy-start = (bf16[2048,512]{1,0:T(8,128)(2,1)S(1)}, bf16[2048,512]{1,0:T(8,128)(2,1)}, u32[]{:S(2)}) copy-start(bf16[2048,512]{1,0:T(8,128)(2,1)} %param.11) | copy-start | bytes 6291460
  2.3 34.1 %copy-start.18 = (f32[512]{0:T(512)}, f32[512]{0:T(512)S(1)}, u32[]{:S(2)}) copy-start(f32[512]{0:T(512)S(1)} %get-tuple-element.39) | copy-start | bytes 6148
  4.2 1.6 copy-start.13
  5.0 2.4 %copy-start.6 = (bf16[7,12,8,2048]{3,2,1,0:T(8,128)(2,1)}, bf16[7,12,8,2048]{3,2,1,0:T(8,128)(2,1)S(1)}, u32[]{:S(2)}) copy-start(bf16[7,12,8,2048]{3,2,1,0:T(8,128)(2,1)S(1)} %pad.7.clone) | copy-start | bytes 8257540
  7.4 10.0 %copy-start.7 = (f32[672,512]{1,0:T(8,128)}, f32[672,512]{1,0:T(8,128)S(1)}, u32[]{:S(2)}) copy-start(f32[672,512]{1,0:T(8,128)S(1)} %get-tuple-element.51) | copy-start | bytes 4128772
  18.0 2.3 %copy-start.2 = (bf16[4608,512]{1,0:T(8,128)(2,1)S(1)}, bf16[4608,512]{1,0:T(8,128)(2,1)}, u32[]{:S(2)}) copy-start(bf16[4608,512]{1,0:T(8,128)(2,1)} %weights.3) | copy-start | bytes 14155780
  25.8 1.5 copy-start.5
  27.3 8.4 %copy-start.15 = (f32[3072]{0:T(1024)S(1)}, f32[3072]{0:T(1024)}, u32[]{:S(2)}) copy-start(f32[3072]{0:T(1024)} %param.12) | copy-start | bytes 36868
  36.4 3.3 %copy-start.16 = (f32[512]{0:T(512)}, f32[512]{0:T(512)S(1)}, u32[]{:S(2)}) copy-start(f32[512]{0:T(512)S(1)} %get-tuple-element.36) | copy-start | bytes 6148
  36.9 5.8 %copy-start.12 = (bf16[672,512]{1,0:T(8,128)(2,1)}, bf16[672,512]{1,0:T(8,128)(2,1)S(1)}, u32[]{:S(2)}) copy-start(bf16[672,512]{1,0:T(8,128)(2,1)S(1)} %select_convert_fusion.3.hidden_two) | copy-start | bytes 2064388
  42.7 12.9 %slice-start = ((f32[3072]{0:T(1024)}), f32[2048]{0:T(1024)S(1)}, s32[]{:S(2)}) async-start(f32[3072]{0:T(1024)} %param.13), calls=%async_computation | async-start | bytes 16384 | tf_op jit(solution)/shard_map/slice | solution.py:411
  73.1 5.2 %copy-start.17 = (f32[512]{0:T(512)S(1)}, f32[512]{0:T(512)}, u32[]{:S(2)}) copy-start(f32[512]{0:T(512)} %copy-done.16) | copy-start | bytes 6148
  73.1 5.2 %copy-start.19 = (f32[512]{0:T(512)S(1)}, f32[512]{0:T(512)}, u32[]{:S(2)}) copy-start(f32[512]{0:T(512)} %copy-done.18) | copy-start | bytes 6148
  78.3 3.2 %copy-start.10 = (bf16[672,2048]{1,0:T(8,128)(2,1)}, bf16[672,2048]{1,0:T(8,128)(2,1)S(1)}, u32[]{:S(2)}) copy-start(bf16[672,2048]{1,0:T(8,128)(2,1)S(1)} %select_convert_fusion.grad_three) | copy-start | bytes 8257540
  78.3 11.4 %copy-start.21 = (f32[512]{0:T(512)S(1)}, f32[512]{0:T(512)}, u32[]{:S(2)}) copy-start(f32[512]{0:T(512)} %get-tuple-element.35) | copy-start | bytes 6148
  91.5 2.3 %copy-start.3 = (bf16[4608,512]{1,0:T(8,128)(2,1)S(1)}, bf16[4608,512]{1,0:T(8,128)(2,1)}, u32[]{:S(2)}) copy-start(bf16[4608,512]{1,0:T(8,128)(2,1)} %weights.3) | copy-start | bytes 14155780
  93.8 6.4 %copy-start.4 = (bf16[672,512]{1,0:T(8,128)(2,1)}, bf16[672,512]{1,0:T(8,128)(2,1)S(1)}, u32[]{:S(2)}) copy-start(bf16[672,512]{1,0:T(8,128)(2,1)S(1)} %select_convert_fusion.2.field.grad_two) | copy-start | bytes 2064388
  93.8 6.4 %copy-start.8 = (f32[672,512]{1,0:T(8,128)S(1)}, f32[672,512]{1,0:T(8,128)}, u32[]{:S(2)}) copy-start(f32[672,512]{1,0:T(8,128)} %copy-done.7) | copy-start | bytes 4128772
  100.2 10.0 %copy-start.20 = (f32[512]{0:T(512)S(1)}, f32[512]{0:T(512)}, u32[]{:S(2)}) copy-start(f32[512]{0:T(512)} %get-tuple-element.34) | copy-start | bytes 6148
  110.3 2.0 copy-start.14
  112.3 4.5 %copy-start.11 = (bf16[672,512]{1,0:T(8,128)(2,1)}, bf16[672,512]{1,0:T(8,128)(2,1)S(1)}, u32[]{:S(2)}) copy-start(bf16[672,512]{1,0:T(8,128)(2,1)S(1)} %select_convert_fusion.1.grad_one) | copy-start | bytes 2064388
  112.3 5.2 %copy-start.9 = (bf16[672,2048]{1,0:T(8,128)(2,1)S(1)}, bf16[672,2048]{1,0:T(8,128)(2,1)}, u32[]{:S(2)}) copy-start(bf16[672,2048]{1,0:T(8,128)(2,1)} %get-tuple-element.28) | copy-start | bytes 8257540
  139.2 94.5 %copy-start.1 = (bf16[2048,512]{1,0:T(8,128)(2,1)S(1)}, bf16[2048,512]{1,0:T(8,128)(2,1)}, u32[]{:S(2)}) copy-start(bf16[2048,512]{1,0:T(8,128)(2,1)} %param.11) | copy-start | bytes 6291460
